TPU v7x, 32 devices: a whole 2x2x4 slice. The times are simulated.
32 devices in a mesh: tp: 4 (over z), ep: 8 (over y, x, core).
Axes of the slice: x: 2, y: 2, z: 4, core: 2. Of those that a mesh axis runs over, the one named last changes fastest.
Arguments:
- x_in: bfloat16 [24, 1024, 2048], P('ep', 'tp')
- topk_idx: int32 [24, 1024, 6], P('ep', 'tp')
- top_gate: float32 [24, 1024, 6], P('ep', 'tp')
- g_attn: bfloat16 [2048], replicated
- w_q: bfloat16 [2048, 3072], P(None, 'tp')
- w_dkv: bfloat16 [2048, 576], replicated
- g_kv: bfloat16 [512], replicated
- w_ukv: bfloat16 [512, 4096], P(None, 'tp')
- w_o: bfloat16 [2048, 2048], P('tp')
- g_ffn: bfloat16 [2048], replicated
- w_gate: bfloat16 [64, 2048, 1408], P(('tp', 'ep'))
- w_up: bfloat16 [64, 2048, 1408], P(('tp', 'ep'))
- w_down: bfloat16 [64, 1408, 2048], P(('tp', 'ep'))
- ws_gate: bfloat16 [2048, 2816], replicated
- ws_up: bfloat16 [2048, 2816], replicated
- ws_down: bfloat16 [2816, 2048], replicated
Outputs:
- output 1: bfloat16 [24, 1024, 2048], P('ep', 'tp')
- output 2: bfloat16 [24, 1024, 576], P('ep', 'tp')
All inputs are finite; a program needn't handle non-finite values.
Results may differ from a plain program's by a relative error of at most 0.0137867.
Values are sent between devices in bfloat16 or wider.
A program may use at most 1 GiB of HBM per device.

v0:
```python
import jax
import jax.numpy as jnp
from jax import lax
from jax.sharding import PartitionSpec as P


def rms_norm(values, gain_vec):
    values32 = values.astype(jnp.float32)
    inv_rms = lax.rsqrt(jnp.mean(values32 * values32, axis=-1, keepdims=True) + 1e-6)
    return (values32 * inv_rms * gain_vec.astype(jnp.float32)).astype(jnp.bfloat16)


def rope_tables(positions, rope_dim):
    half_dim = rope_dim // 2
    inv_freq = 10000.0 ** (-2.0 * jnp.arange(half_dim, dtype=jnp.float32) / rope_dim)
    angles = positions.astype(jnp.float32)[:, None] * inv_freq[None, :]
    return jnp.cos(angles), jnp.sin(angles)


def rotate(values, cos_tab, sin_tab):
    half_dim = values.shape[-1] // 2
    first = values[..., :half_dim].astype(jnp.float32)
    second = values[..., half_dim:].astype(jnp.float32)
    return jnp.concatenate([first * cos_tab - second * sin_tab, second * cos_tab + first * sin_tab], axis=-1).astype(jnp.bfloat16)


def model_dims(w_q, w_dkv, g_kv, w_ukv, w_o):
    kv_rank = g_kv.shape[0]
    rope_dim = w_dkv.shape[1] - kv_rank
    heads = (w_q.shape[1] - w_ukv.shape[1] + w_o.shape[0]) // rope_dim
    return kv_rank, rope_dim, heads, w_q.shape[1] // heads - rope_dim, w_o.shape[0] // heads


def attend(query, key_val, k_rope, q_cos, q_sin, causal, nope_dim):
    rope_dim = k_rope.shape[-1]
    q_rope = rotate(query[..., nope_dim:], q_cos[:, None, :], q_sin[:, None, :])
    scores = jnp.einsum('bqhd,bkhd->bhqk', query[..., :nope_dim], key_val[..., :nope_dim], preferred_element_type=jnp.float32)
    scores = scores + jnp.einsum('crie,cle->cirl', q_rope, k_rope, preferred_element_type=jnp.float32)
    scores = jnp.where(causal, scores * (nope_dim + rope_dim) ** -0.5, -jnp.inf)
    attn_prob = jax.nn.softmax(scores, axis=-1).astype(jnp.bfloat16)
    return jnp.einsum('bhqk,bkhd->bqhd', attn_prob, key_val[..., nope_dim:], preferred_element_type=jnp.float32).astype(jnp.bfloat16)


def moe_block(hidden, ids_loc, gate_loc, g_ffn, w_gate, w_up, w_down, ws_gate, ws_up, ws_down, expert_count, dev_count):
    bat_loc, seq_loc, width = hidden.shape
    tok_dev = bat_loc * seq_loc
    top_k = ids_loc.shape[-1]
    capacity = 3 * (tok_dev * top_k // expert_count)
    local_experts = expert_count // dev_count
    normed = rms_norm(hidden, g_ffn).reshape(tok_dev, width)
    flat_ids = ids_loc.reshape(tok_dev * top_k)
    onehot = (flat_ids[:, None] == jnp.arange(expert_count)[None, :]).astype(jnp.int32)
    slot_rank = jnp.sum(jnp.cumsum(onehot, axis=0) * onehot, axis=1) - 1
    slot_ids = flat_ids * capacity + slot_rank
    token_of_slot = jnp.full((expert_count * capacity,), tok_dev, jnp.int32).at[slot_ids].set(jnp.arange(tok_dev * top_k, dtype=jnp.int32) // top_k)
    padded = jnp.concatenate([normed, jnp.zeros((1, width), jnp.bfloat16)], axis=0)
    send_buf = padded[token_of_slot].reshape(dev_count, local_experts * capacity, width)
    recv_buf = lax.all_to_all(send_buf, ('tp', 'ep'), 0, 0, tiled=True).reshape(dev_count, local_experts, capacity, width)
    act_gate = jnp.einsum('necd,edf->necf', recv_buf, w_gate, preferred_element_type=jnp.float32)
    act_up = jnp.einsum('necd,edf->necf', recv_buf, w_up, preferred_element_type=jnp.float32)
    act_hidden = (jax.nn.silu(act_gate) * act_up).astype(jnp.bfloat16)
    expert_out = jnp.einsum('necf,efd->necd', act_hidden, w_down, preferred_element_type=jnp.float32).astype(jnp.bfloat16)
    expert_out = expert_out.reshape(dev_count, local_experts * capacity, width)
    returned = lax.all_to_all(expert_out, ('tp', 'ep'), 0, 0, tiled=True).reshape(expert_count * capacity, width)
    picked = returned[slot_ids].reshape(tok_dev, top_k, width)
    routed = jnp.sum(gate_loc.reshape(tok_dev, top_k, 1) * picked.astype(jnp.float32), axis=1)
    shared_gate = jnp.dot(normed, ws_gate, preferred_element_type=jnp.float32)
    shared_up = jnp.dot(normed, ws_up, preferred_element_type=jnp.float32)
    shared_act = (jax.nn.silu(shared_gate) * shared_up).astype(jnp.bfloat16)
    shared_out = jnp.dot(shared_act, ws_down, preferred_element_type=jnp.float32)
    y_sum = hidden.reshape(tok_dev, width).astype(jnp.float32) + routed + shared_out
    return y_sum.astype(jnp.bfloat16).reshape(bat_loc, seq_loc, width)


def solution(mesh):
    tp_size = mesh.shape['tp']
    ep_size = mesh.shape['ep']
    dev_count = tp_size * ep_size
    token_spec = P('ep', 'tp', None)
    expert_spec = P(('tp', 'ep'), None, None)
    in_specs = (token_spec, token_spec, token_spec, P(None), P(None, 'tp'), P(None, None), P(None), P(None, 'tp'), P('tp', None), P(None), expert_spec, expert_spec, expert_spec, P(None, None), P(None, None), P(None, None))

    def layer(x_in, topk_idx, top_gate, g_attn, w_q, w_dkv, g_kv, w_ukv, w_o, g_ffn, w_gate, w_up, w_down, ws_gate, ws_up, ws_down):
        kv_rank, rope_dim, heads, nope_dim, value_dim = model_dims(w_q, w_dkv, g_kv, w_ukv, w_o)
        expert_count = w_gate.shape[0]

        def device_layer(x_loc, ids_loc, gate_loc, g_attn, w_q, w_dkv, g_kv, w_ukv, w_o, g_ffn, w_gate, w_up, w_down, ws_gate, ws_up, ws_down):
            bat_loc, seq_loc, width = x_loc.shape
            seq_len = seq_loc * tp_size
            heads_loc = w_o.shape[0] // value_dim
            tp_index = lax.axis_index('tp')
            normed = rms_norm(x_loc, g_attn)
            normed_full = lax.all_gather(normed, 'tp', axis=1, tiled=True)
            query = jnp.einsum('bsd,dn->bsn', normed_full, w_q, preferred_element_type=jnp.float32).astype(jnp.bfloat16).reshape(bat_loc, seq_len, heads_loc, nope_dim + rope_dim)
            latent = jnp.einsum('bsd,dn->bsn', normed_full, w_dkv, preferred_element_type=jnp.float32)
            cos_tab, sin_tab = rope_tables(jnp.arange(seq_len), rope_dim)
            c_kv = rms_norm(latent[..., :kv_rank], g_kv)
            k_rope = rotate(latent[..., kv_rank:], cos_tab, sin_tab)
            cache_full = jnp.concatenate([c_kv, k_rope], axis=-1)
            cache_loc = lax.dynamic_slice_in_dim(cache_full, tp_index * seq_loc, seq_loc, axis=1)
            key_val = jnp.einsum('bsr,rn->bsn', c_kv, w_ukv, preferred_element_type=jnp.float32).astype(jnp.bfloat16).reshape(bat_loc, seq_len, heads_loc, nope_dim + value_dim)
            causal = jnp.arange(seq_len)[:, None] >= jnp.arange(seq_len)[None, :]
            heads_out = attend(query, key_val, k_rope, cos_tab, sin_tab, causal, nope_dim).reshape(bat_loc, seq_len, heads_loc * value_dim)
            partial_out = jnp.einsum('bsn,nd->bsd', heads_out, w_o, preferred_element_type=jnp.float32).astype(jnp.bfloat16)
            attn = lax.psum_scatter(partial_out, 'tp', scatter_dimension=1, tiled=True)
            hidden = (x_loc.astype(jnp.float32) + attn.astype(jnp.float32)).astype(jnp.bfloat16)
            y_loc = moe_block(hidden, ids_loc, gate_loc, g_ffn, w_gate, w_up, w_down, ws_gate, ws_up, ws_down, expert_count, dev_count)
            return y_loc, cache_loc

        return jax.shard_map(device_layer, mesh=mesh, in_specs=in_specs, out_specs=(token_spec, token_spec), check_vma=False)(x_in, topk_idx, top_gate, g_attn, w_q, w_dkv, g_kv, w_ukv, w_o, g_ffn, w_gate, w_up, w_down, ws_gate, ws_up, ws_down)

    return layer
```

profile of v0, /device:TPU:25, one launch (start us, length us, event | category | flops | bytes accessed | tf_op | source)
XLA Modules:
  0.0 3611.4 jit_solution(18331780545021856684)
XLA Ops:
  7.2 2.7 fusion.18
  10.7 4.3 fusion.20
  15.1 1.3 iota_compare_fusion
  16.4 1.2 multiply_cosine_fusion
  17.7 214.5 %all-gather.2.cloned.1.call-done = bf16[3,1024,2048]{2,1,0:T(8,128)(2,1)} async-done(((bf16[3,256,2048]{2,1,0:T(8,128)(2,1)}), bf16[3,1024,2048]{2,1,0:T(8,128)(2,1)}) %all-gather.2.cloned.1.call-update) | async-done | bytes 12582928 | tf_op jit(solution)/shard_map/all_gather | solution.py:93
  232.1 11.4 fusion.35
  243.6 0.8 multiply_reduce_fusion.2
  244.7 14.7 fusion.32
  259.3 2.0 fusion.42
  261.4 1.0 multiply_convert_fusion.2
  262.4 5.7 convolution_convert_fusion.1
  268.2 19.5 fusion.45
  287.7 41.0 %fusion.66 = (f32[3,4,1024]{2,1,0:T(4,128)S(1)}, f32[3,4,1024,1024]{2,3,1,0:T(8,128)}) fusion(f32[3,1024,1024,4]{2,1,3,0:T(8,128)} %fusion.45, pred[1024,1024]{0,1:T(8,128)(4,1)S(1)} %copy-done.14, bf16[3,1024,4,256]{1,3,2,0:T(8,128)(2,1)} %bitcast.135, bf16[3,1024,4,192]{1,3,2,0:T(8,128)(2,1)} %bitcast.131), kind=kOutput, calls=%fused_computation.112 | convolution fusion | flops 3284141056 | bytes 108052480 | tf_op jit(solution)/shard_map/sub | solution.py:40
  328.8 17.8 fusion.37
  346.6 9.7 convolution_convert_fusion
  356.3 0.7 copy-done.15
  357.5 0.9 eq.25
  358.3 1.2 fusion.49
  359.5 35.8 reduce-window.6
  395.3 2.8 slice.58
  398.1 1.9 copy.51
  399.9 0.8 reduce-window.9
  401.4 0.9 copy.33
  402.3 0.9 mul.281
  403.2 1.6 broadcast_add_fusion
  404.8 1.0 fusion.51
  405.8 0.8 fusion.62
  406.6 17.4 scatter_custom_fusion
  424.1 144.1 %reduce-scatter.2.cloned.1.call-done = bf16[3,256,2048]{2,1,0:T(8,128)(2,1)} async-done(((bf16[3,1024,2048]{2,1,0:T(8,128)(2,1)}), bf16[3,256,2048]{2,1,0:T(8,128)(2,1)}) %reduce-scatter.2.cloned.1.call-update) | async-done | bytes 3145744 | tf_op jit(solution)/shard_map/reduce_scatter | solution.py:105
  568.2 5.6 fusion.26
  573.8 1.8 multiply_convert_fusion.1
  575.6 1.7 copy-done.3
  577.6 51.9 %gather_fusion = bf16[13824,2048]{1,0:T(8,128)(2,1)} fusion(bf16[769,2048]{1,0:T(8,128)(2,1)S(1)} %concatenate.17, s32[14336]{0:T(1024)S(1)} %pad_clamp_fusion), kind=kCustom, calls=%fused_computation | custom fusion | bytes 113301504 | tf_op jit(solution)/shard_map/gather | solution.py:57
  629.5 1254.0 %all_to_all.10 = bf16[32,432,2048]{2,1,0:T(8,128)(2,1)} all-to-all(bf16[32,432,2048]{2,1,0:T(8,128)(2,1)} %bitcast.123), channel_id=1, replica_groups=mesh['tp'=4,'ep'=8] {'tp','ep'}, dimensions={0} | all-to-all | bytes 113246208 | tf_op jit(solution)/shard_map/all_to_all | solution.py:58
  1883.5 98.2 %fusion.7 = f32[2,32,216,1408]{3,2,1,0:T(8,128)} fusion(bf16[32,2,216,2048]{3,2,1,0:T(8,128)(2,1)} %bitcast.124, bf16[2,2048,1408]{2,1,0:T(8,128)(2,1)} %param.27), kind=kOutput, calls=%fused_computation.18 | convolution fusion | flops 79725330432 | bytes 146014208 | tf_op jit(solution)/shard_map/necd,edf->necf/dot_general | solution.py:60
  1981.7 106.6 %fusion.1.clone.4 = bf16[32,2,216,1408]{3,2,0,1:T(8,128)(2,1)} fusion(f32[2,32,216,1408]{3,2,1,0:T(8,128)} %fusion.7, bf16[32,2,216,2048]{3,2,1,0:T(8,128)(2,1)} %bitcast.125, bf16[2,2048,1408]{2,1,0:T(8,128)(2,1)} %param.26), kind=kOutput, calls=%fused_computation.5.clone.clone.clone.1 | convolution fusion | flops 79842115584 | bytes 184942592 | tf_op jit(solution)/shard_map/necd,edf->necf/dot_general | solution.py:59
  2088.3 96.9 %convert_bitcast_fusion = bf16[32,2,216,2048]{3,2,0,1:T(8,128)(2,1)} fusion(bf16[2,1408,2048]{2,1,0:T(8,128)(2,1)} %param.28, bf16[32,2,216,1408]{3,2,0,1:T(8,128)(2,1)} %fusion.1.clone.4), kind=kOutput, calls=%fused_computation.11 | convolution fusion | flops 79753641984 | bytes 107085824 | tf_op jit(solution)/shard_map/necf,efd->necd/dot_general | solution.py:62
  2185.2 37.8 %copy.39 = bf16[32,2,216,2048]{3,2,1,0:T(8,128)(2,1)} copy(bf16[32,2,216,2048]{3,2,0,1:T(8,128)(2,1)} %convert_bitcast_fusion) | data formatting | bytes 113246208 | tf_op jit(solution)/shard_map/convert_element_type | solution.py:62
  2223.0 5.8 all-to-all-start.1
  2228.8 1.7 copy.32
  2230.5 1.3 pad_clamp_fusion.1
  2231.8 2.1 fusion.54
  2234.0 14.8 fusion.71
  2248.7 1221.9 %all-to-all-done.1 = bf16[32,432,2048]{2,1,0:T(8,128)(2,1)} async-done(((bf16[32,432,2048]{2,1,0:T(8,128)(2,1)}), bf16[32,432,2048]{2,1,0:T(8,128)(2,1)}, u32[]{:S(2)}, u32[]{:S(2)}) %all-to-all-start.1) | async-done | bytes 56623136 | tf_op jit(solution)/shard_map/all_to_all | solution.py:64
  3470.6 46.9 %gather_fusion.1 = bf16[4608,2048]{1,0:T(8,128)(2,1)} fusion(bf16[13824,2048]{1,0:T(8,128)(2,1)} %bitcast.29, s32[5120]{0:T(1024)S(1)} %copy-done.16), kind=kCustom, calls=%fused_computation.1 | custom fusion | bytes 37767168 | tf_op jit(solution)/shard_map/gather | solution.py:65
  3517.5 32.5 reshape.247
  3550.0 23.5 multiply_reduce_fusion
  3573.5 30.8 fusion.23
  (63 shorter events, 2.5 us)
Async XLA Ops:
  7.2 237.5 %copy-start = (bf16[2048,768]{1,0:T(8,128)(2,1)S(1)}, bf16[2048,768]{1,0:T(8,128)(2,1)}, u32[]{:S(2)}) copy-start(bf16[2048,768]{1,0:T(8,128)(2,1)} %param.20) | copy-start | bytes 9437188
  7.2 7.9 copy-start.19
  7.2 224.9 %all-gather.2.cloned.1.call-start = ((), (), s32[]{:S(2)}) async-start(), calls=%async_computation.3 | async-start | bytes 15728640 | tf_op jit(solution)/shard_map/all_gather | solution.py:93
  15.0 553.1 %reduce-scatter.2.cloned.1.call-start = ((), (), s32[]{:S(2)}) async-start(), calls=%async_computation.4 | async-start | bytes 15728640 | tf_op jit(solution)/shard_map/reduce_scatter | solution.py:105
  243.5 0.9 copy-start.12
  243.6 1.0 copy-start.13
  244.6 23.5 copy-start.7
  244.7 23.5 copy-start.9
  259.3 3.1 copy-start.21
  262.4 5.7 copy-start.6
  268.2 19.6 copy-start.14
  328.8 17.9 copy-start.20
  356.3 0.7 copy-start.15
  356.3 2.0 copy-start.18
  359.5 208.7 %copy-start.2 = (bf16[3,256,2048]{2,1,0:T(8,128)(2,1)S(1)}, bf16[3,256,2048]{2,1,0:T(8,128)(2,1)}, u32[]{:S(2)}) copy-start(bf16[3,256,2048]{2,1,0:T(8,128)(2,1)} %param.16) | copy-start | bytes 9437188
  406.6 17.4 copy-start.17
  568.2 5.7 copy-start.5
  575.6 1.7 copy-start.3
  2222.9 8.9 copy-start.8
  2223.0 8.9 copy-start.10
  2223.0 11.0 copy-start.4
  2223.0 1247.6 %all-to-all-start.1 = ((bf16[32,432,2048]{2,1,0:T(8,128)(2,1)}), bf16[32,432,2048]{2,1,0:T(8,128)(2,1)}, u32[]{:S(2)}, u32[]{:S(2)}) async-start(bf16[32,432,2048]{2,1,0:T(8,128)(2,1)} %bitcast.122), calls=%async_computation.2 | async-start | bytes 113246208 | tf_op jit(solution)/shard_map/all_to_all | solution.py:64
  2234.0 1236.7 %copy-start.16 = (s32[5120]{0:T(1024)S(1)}, s32[5120]{0:T(1024)}, u32[]{:S(2)}) copy-start(s32[5120]{0:T(1024)} %pad_clamp_fusion.1) | copy-start | bytes 61444
  3517.5 32.5 copy-start.11
  3573.5 30.8 copy-start.1
Sparse Core Ops, SparseCore 0:
  15.2 216.9 all-gather.1
  356.4 211.6 reduce-scatter.1
where the time goes:
time: 3620 us; the launch traced here: 3610 us
  waiting for transfers between devices  1580 us (44%)
  blocking collectives  1250 us (35%)
  matrix products  467 us (13%)
  local copies, waits for them, and re-layouts  199 us (5%)
  other arithmetic  90.5 us (2%)
    all_to_all x1, blocking collectives, moe_block(): lax.all_to_all(send_buf, ('tp', 'ep'), 0, 0, tiled=True)  1250 us
    all_to_all x1, waiting for transfers between devices, moe_block(): lax.all_to_all(expert_out, ('tp', 'ep'), 0, 0, tiled=True)  1220 us
    all_gather x1, waiting for transfers between devices, device_layer(): normed_full = lax.all_gather(normed, 'tp', axis=1, tiled=True)  214 us
    reduce_scatter x1, waiting for transfers between devices, device_layer(): attn = lax.psum_scatter(partial_out, 'tp', scatter_dimension=1, tiled=True)  144 us
    dot_general x1, matrix products, moe_block(): jnp.einsum('necd,edf->necf', recv_buf, w_gate, preferred_element_type=jnp...  107 us
    dot_general x1, matrix products, moe_block(): jnp.einsum('necd,edf->necf', recv_buf, w_up, preferred_element_type=jnp.f...  98.2 us
    dot_general x1, matrix products, moe_block(): jnp.einsum('necf,efd->necd', act_hidden, w_down, preferred_element_type=j...  96.9 us
  transfers between devices with their start and end apart: 3, of which 3 were waited for; matrix products, arithmetic and copies ran while one was open for 2% of the time, Pallas kernels for 0%

commit v1 on v0

v1 whole, which is shorter than its diff:
```python
import functools

import jax
import jax.numpy as jnp
from jax import lax
from jax.experimental import pallas as pl
from jax.experimental.pallas import tpu as pltpu
from jax.sharding import PartitionSpec as P


F32 = jnp.float32
BF16 = jnp.bfloat16
VMEM_MAX = 67043328
SMALL = 32


def rms_norm(values, gain_vec):
    values32 = values.astype(F32)
    inv_rms = lax.rsqrt(jnp.mean(values32 * values32, axis=-1, keepdims=True) + 1e-6)
    return (values32 * inv_rms * gain_vec.astype(F32)).astype(BF16)


def rope_tables(positions, rope_dim):
    half_dim = rope_dim // 2
    inv_freq = 10000.0 ** (-2.0 * jnp.arange(half_dim, dtype=F32) / rope_dim)
    angles = positions.astype(F32)[:, None] * inv_freq[None, :]
    return jnp.cos(angles), jnp.sin(angles)


def rotate(values, cos_tab, sin_tab):
    half_dim = values.shape[-1] // 2
    first = values[..., :half_dim].astype(F32)
    second = values[..., half_dim:].astype(F32)
    return jnp.concatenate([first * cos_tab - second * sin_tab, second * cos_tab + first * sin_tab], axis=-1).astype(BF16)


def model_dims(w_q, w_dkv, g_kv, w_ukv, w_o):
    kv_rank = g_kv.shape[0]
    rope_dim = w_dkv.shape[1] - kv_rank
    heads = (w_q.shape[1] - w_ukv.shape[1] + w_o.shape[0]) // rope_dim
    return kv_rank, rope_dim, heads, w_q.shape[1] // heads - rope_dim, w_o.shape[0] // heads


def dot32(lhs, rhs):
    return jnp.dot(lhs, rhs, preferred_element_type=F32)


def project_body(first, u_ref, w_ref, o_ref):
    depth, cols = w_ref.shape[1], o_ref.shape[2]
    total = jnp.zeros(o_ref.shape[1:], F32)
    for part in range(u_ref.shape[1] // depth):
        total = total + dot32(u_ref[:, part * depth:(part + 1) * depth], w_ref[0, :, first + part * cols:first + (part + 1) * cols])
    o_ref[0] = total.astype(BF16)


def project(rows, packed, first, cols):
    toks, width = rows.shape
    groups, depth, wide = packed.shape
    return pl.pallas_call(
        functools.partial(project_body, first),
        grid=(groups,),
        in_specs=[pl.BlockSpec((toks, width), lambda g: (0, 0)), pl.BlockSpec((1, depth, wide), lambda g: (g, 0, 0))],
        out_specs=pl.BlockSpec((1, toks, cols), lambda g: (g, 0, 0)),
        out_shape=jax.ShapeDtypeStruct((groups, toks, cols), BF16),
        cost_estimate=pl.CostEstimate(flops=2 * toks * width * groups * cols, bytes_accessed=20_000_000, transcendentals=0),
        name="project",
    )(rows, packed)


def attend_body(nope, rope, vdim, rank, z_ref, q_ref, c0, c1, c2, c3, w_ref, cos_ref, sin_ref, o_ref):
    rows, blk = q_ref.shape[1], c0.shape[1]
    scale = (nope + rope) ** -0.5
    cache = jnp.concatenate([c0[0], c1[0], c2[0], c3[0]], axis=0)
    key_val = dot32(cache[:, :rank], w_ref[0]).astype(BF16)
    k_rope = cache[:, rank:]
    keys = 4 * blk
    key_idx = lax.broadcasted_iota(jnp.int32, (1, keys), 1)
    ahead = key_idx // blk
    plane = z_ref[0] + ahead
    plane = jnp.where(plane >= 4, plane - 4, plane)
    key_pos = plane * blk + key_idx - ahead * blk
    row_pos = z_ref[0] * blk + lax.broadcasted_iota(jnp.int32, (rows, keys), 0)
    causal = row_pos >= key_pos
    cos_tab, sin_tab = cos_ref[...], sin_ref[...]
    contract = (((1,), (1,)), ((), ()))
    for head in range(2):
        base = head * (nope + rope)
        q_nope = q_ref[0, :, base:base + nope]
        q_rope = rotate(q_ref[0, :, base + nope:base + nope + rope], cos_tab, sin_tab)
        start = head * (nope + vdim)
        k_nope, value = key_val[:, start:start + nope], key_val[:, start + nope:start + nope + vdim]
        scores = lax.dot_general(q_nope, k_nope, contract, preferred_element_type=F32)
        scores = scores + lax.dot_general(q_rope, k_rope, contract, preferred_element_type=F32)
        scores = jnp.where(causal, scores * scale, -jnp.inf)
        unnorm = jnp.exp(scores - jnp.max(scores, axis=-1, keepdims=True))
        prob = (unnorm * (1.0 / jnp.sum(unnorm, axis=-1, keepdims=True))).astype(BF16)
        o_ref[:, head * vdim:(head + 1) * vdim] = dot32(prob, value).astype(BF16)


def attend(query, caches, packed, z_one, cos_tab, sin_tab, dims):
    rank, rope, heads, nope, vdim = dims
    bat, blk, wide = caches[0].shape
    _, toks, qcols = query.shape
    rows = toks // bat
    pair = 2 * (nope + rope)
    per = qcols // pair
    kv_cols = 2 * (nope + vdim)
    body = functools.partial(attend_body, nope, rope, vdim, rank)
    return pl.pallas_call(
        body,
        grid=(heads // 2, bat),
        in_specs=[
            pl.BlockSpec(memory_space=pltpu.SMEM),
            pl.BlockSpec((1, rows, pair), lambda h, b: (h // per, b, h % per)),
        ] + [pl.BlockSpec((1, blk, wide), lambda h, b: (b, 0, 0))] * 4 + [
            pl.BlockSpec((1, rank, kv_cols), lambda h, b: (h // per, 0, h % per)),
            pl.BlockSpec((rows, rope // 2), lambda h, b: (0, 0)),
            pl.BlockSpec((rows, rope // 2), lambda h, b: (0, 0)),
        ],
        out_specs=pl.BlockSpec((rows, 2 * vdim), lambda h, b: (b, h)),
        out_shape=jax.ShapeDtypeStruct((toks, heads * vdim), BF16),
        cost_estimate=pl.CostEstimate(flops=60_000_000_000, bytes_accessed=40_000_000, transcendentals=0),
        name="attend",
    )(z_one, query, *caches, packed, cos_tab, sin_tab)


def experts_body(half, small_ref, ids_ref, *refs):
    toks, (gate_a, up_a, down_a, gate_b, up_b, down_b) = refs[:8], refs[8:14]
    outs = refs[14:18]
    tok, gate_up, down, stage, few, tok_sem, in_sem, down_sem, out_sem = refs[18:]
    step = pl.program_id(0)
    width = gate_a.shape[2]
    cap = stage.shape[1]
    tok_count = tok.shape[1]

    def load_gate_up(which):
        slot = which % 2
        src = (gate_a, up_a) if which < 2 else (gate_b, up_b)
        for part in range(2):
            pltpu.make_async_copy(src[part].at[which % 2], gate_up.at[slot, :, part * width:(part + 1) * width], in_sem.at[slot, part]).start()

    def load_down(which):
        src = down_a if which < 2 else down_b
        pltpu.make_async_copy(src.at[which % 2], down.at[which % 2], down_sem.at[which % 2]).start()

    @pl.when(step == 0)
    def _():
        load_gate_up(0)
        for index in range(8):
            pltpu.make_async_copy(toks[index], tok.at[index // 2, (index % 2) * half:(index % 2 + 1) * half], tok_sem.at[index]).start()
        load_down(0)

    for which in range(1, 4):
        @pl.when(step == which - 1)
        def _():
            load_gate_up(which)
            load_down(which)

    @pl.when(step == 0)
    def _():
        for index in range(8):
            pltpu.make_async_copy(toks[index], tok.at[index // 2, (index % 2) * half:(index % 2 + 1) * half], tok_sem.at[index]).wait()

    for which in range(4):
        @pl.when(step == which)
        def _():
            slot = which % 2
            for part in range(2):
                pltpu.make_async_copy(gate_a.at[0], gate_up.at[slot, :, part * width:(part + 1) * width], in_sem.at[slot, part]).wait()
            pltpu.make_async_copy(down_a.at[0], down.at[slot], down_sem.at[slot]).wait()

    now = lax.rem(step, 2)

    def mlp(rows):
        both = dot32(rows, gate_up[now])
        hidden = (jax.nn.silu(both[:, :width]) * both[:, width:]).astype(BF16)
        return dot32(hidden, down[now]).astype(BF16)

    def pick(home, count):
        ids = ids_ref[home, :count, :]
        lane = lax.broadcasted_iota(jnp.int32, ids.shape, 1)
        parts = [jnp.where(ids == lane + 128 * blk, 1.0, 0.0).astype(BF16) for blk in range(tok_count // 128)]
        return dot32(jnp.concatenate(parts, axis=1), tok[home]).astype(BF16)

    is_small = small_ref[step] == 1

    @pl.when(is_small)
    def _():
        few[...] = mlp(jnp.concatenate([pick(home, SMALL) for home in range(4)], axis=0))

    @pl.loop(0, 4)
    def _(home):
        slot = lax.rem(home, 2)

        @pl.when(jnp.logical_or(step > 0, home >= 2))
        def _():
            pltpu.make_async_copy(stage.at[slot], outs[0].at[0], out_sem.at[slot]).wait()

        @pl.when(is_small)
        def _():
            stage[slot, :SMALL, :] = few[pl.ds(pl.multiple_of(home * SMALL, SMALL), SMALL), :]

        @pl.when(jnp.logical_not(is_small))
        def _():
            stage[slot] = mlp(pick(home, cap))

        for which in range(4):
            @pl.when(home == which)
            def _():
                pltpu.make_async_copy(stage.at[slot], outs[which].at[step], out_sem.at[slot]).start()

    @pl.when(step == 3)
    def _():
        for slot in range(2):
            pltpu.make_async_copy(stage.at[slot], outs[0].at[0], out_sem.at[slot]).wait()


def experts(small, ids, toks, weights, cap):
    half, width = toks[0].shape
    ff = weights[0].shape[2]
    hbm = pl.BlockSpec(memory_space=pl.ANY)
    return pl.pallas_call(
        functools.partial(experts_body, half),
        grid=(4,),
        in_specs=[pl.BlockSpec(memory_space=pltpu.SMEM), pl.BlockSpec((4, cap, 128), lambda e: (e, 0, 0))] + [hbm] * 14,
        out_specs=[hbm] * 4,
        out_shape=[jax.ShapeDtypeStruct((4, cap, width), BF16)] * 4,
        scratch_shapes=[
            pltpu.VMEM((4, 2 * half, width), BF16),
            pltpu.VMEM((2, width, 2 * ff), BF16),
            pltpu.VMEM((2, ff, width), BF16),
            pltpu.VMEM((2, cap, width), BF16),
            pltpu.VMEM((4 * SMALL, width), BF16),
            pltpu.SemaphoreType.DMA((8,)),
            pltpu.SemaphoreType.DMA((2, 2)),
            pltpu.SemaphoreType.DMA((2,)),
            pltpu.SemaphoreType.DMA((2,)),
        ],
        compiler_params=pltpu.CompilerParams(vmem_limit_bytes=VMEM_MAX),
        cost_estimate=pl.CostEstimate(flops=60_000_000_000, bytes_accessed=100_000_000, transcendentals=0),
        name="experts",
    )(small, ids, *toks, *weights)


def combine_body(tok_ref, gate_ref, cnt_ref, r0, r1, r2, r3, *rest):
    extra, (out_ref, acc, turn) = rest[:-3], rest[-3:]
    step = pl.program_id(0)
    cap, width = r0.shape[1], r0.shape[2]
    lanes = width // 128
    toks = out_ref.shape[0]

    @pl.when(step == 0)
    def _():
        acc[...] = jnp.zeros_like(acc)

    for which, src in enumerate((r0, r1, r2, r3)):
        @pl.when(step // 4 == which)
        def _():
            @pl.loop(0, (cnt_ref[step] + 15) // 16)
            def _(group):
                first = pl.multiple_of(group * 16, 16)
                rows = src[0, pl.ds(first, 16), :].astype(F32)
                for blk in range(lanes):
                    turn[pl.ds(blk, 16, stride=lanes), :] = rows[:, 128 * blk:128 * (blk + 1)]
                base = step * cap + first
                for part in range(2):
                    spots = [pl.multiple_of(tok_ref[base + 8 * part + r] * lanes, lanes) for r in range(8)]
                    olds = [acc[pl.ds(spot, lanes), :] for spot in spots]
                    news = [olds[r] + gate_ref[base + 8 * part + r] * turn[(8 * part + r) * lanes:(8 * part + r + 1) * lanes, :] for r in range(8)]
                    for r in range(8):
                        acc[pl.ds(spots[r], lanes), :] = news[r]

    @pl.when(step == 15)
    def _():
        @pl.loop(0, toks // 8)
        def _(tile):
            first = pl.multiple_of(tile * 8, 8)
            for blk in range(lanes):
                value = acc[pl.ds(first * lanes + blk, 8, stride=lanes), :]
                for more in extra:
                    value = value + more[pl.ds(first, 8), 128 * blk:128 * (blk + 1)]
                out_ref[pl.ds(first, 8), 128 * blk:128 * (blk + 1)] = value


def combine(slot_tok, slot_gate, counts, rows, extra, toks):
    cap, width = rows[0].shape[1:]
    lanes = width // 128

    def spec(which):
        return pl.BlockSpec((1, cap, width), lambda i, *_: (jnp.clip(i - 4 * which, 0, 3), 0, 0))

    whole = pl.BlockSpec((toks, width), lambda i, *_: (0, 0))
    return pl.pallas_call(
        combine_body,
        grid_spec=pltpu.PrefetchScalarGridSpec(
            num_scalar_prefetch=3,
            grid=(16,),
            in_specs=[spec(which) for which in range(4)] + [whole] * len(extra),
            out_specs=whole,
            scratch_shapes=[pltpu.VMEM(((toks + 1) * lanes, 128), F32), pltpu.VMEM((16 * lanes, 128), F32)],
        ),
        out_shape=jax.ShapeDtypeStruct((toks, width), F32),
        compiler_params=pltpu.CompilerParams(vmem_limit_bytes=48 * 2**20),
        cost_estimate=pl.CostEstimate(flops=10_000_000_000, bytes_accessed=20_000_000, transcendentals=0),
        name="combine",
    )(slot_tok, slot_gate, counts, *rows, *extra)


def shared_body(rows_ref, gate_ref, up_ref, down_ref, out_ref):
    rows = rows_ref[...]
    hidden = (jax.nn.silu(dot32(rows, gate_ref[...])) * dot32(rows, up_ref[...])).astype(BF16)
    part = dot32(hidden, down_ref[...])

    @pl.when(pl.program_id(0) == 0)
    def _():
        out_ref[...] = part

    @pl.when(pl.program_id(0) > 0)
    def _():
        out_ref[...] += part


def shared_experts(rows, ws_gate, ws_up, ws_down):
    toks, width = rows.shape
    inner = ws_gate.shape[1]
    blk = 256
    return pl.pallas_call(
        shared_body,
        grid=(inner // blk,),
        in_specs=[
            pl.BlockSpec((toks, width), lambda f: (0, 0)),
            pl.BlockSpec((width, blk), lambda f: (0, f)),
            pl.BlockSpec((width, blk), lambda f: (0, f)),
            pl.BlockSpec((blk, width), lambda f: (f, 0)),
        ],
        out_specs=pl.BlockSpec((toks, width), lambda f: (0, 0)),
        out_shape=jax.ShapeDtypeStruct((toks, width), F32),
        cost_estimate=pl.CostEstimate(flops=6 * toks * width * inner, bytes_accessed=50_000_000, transcendentals=0),
        name="shared",
    )(rows, ws_gate, ws_up, ws_down)


def route_slots(ids, gates, expert_count, cap):
    toks = ids.shape[0]
    hits = ids[:, :, None] == jnp.arange(expert_count)[None, None, :]
    member = jnp.any(hits, axis=1)
    gate_of = jnp.sum(jnp.where(hits, gates[:, :, None], 0.0), axis=1)
    earlier = (jnp.arange(toks)[:, None] > jnp.arange(toks)[None, :]).astype(BF16)
    rank = dot32(earlier, member.astype(BF16)).astype(jnp.int32)
    key = jnp.where(member, rank, -1)
    match = key[:, None, :] == jnp.arange(cap)[None, :, None]
    tok_num = (jnp.arange(toks, dtype=F32) - toks)[:, None, None]
    slot_tok = jnp.sum(jnp.where(match, tok_num, 0.0), axis=0) + toks
    slot_gate = jnp.sum(jnp.where(match, gate_of[:, None, :], 0.0), axis=0)
    return jnp.stack([slot_tok.T, slot_gate.T])


def solution(mesh):
    tp_size = mesh.shape['tp']
    ep_size = mesh.shape['ep']
    token_spec = P('ep', 'tp', None)
    expert_spec = P(('tp', 'ep'), None, None)
    in_specs = (token_spec, token_spec, token_spec, P(None), P(None, 'tp'), P(None, None), P(None), P(None, 'tp'), P('tp', None), P(None), expert_spec, expert_spec, expert_spec, P(None, None), P(None, None), P(None, None))
    core, flip_x, flip_y = 1, 2, 4

    def swap(values, mask):
        return lax.ppermute(values, 'ep', [(i, i ^ mask) for i in range(ep_size)])

    def from_plane(values, ahead):
        return lax.ppermute(values, 'tp', [((i + ahead) % tp_size, i) for i in range(tp_size)])

    def to_plane(values, ahead):
        return lax.ppermute(values, 'tp', [(i, (i + ahead) % tp_size) for i in range(tp_size)])

    def gather_weight(shard):
        piece_rows = shard.shape[0] // ep_size
        piece = lax.dynamic_slice_in_dim(shard, lax.axis_index('ep') * piece_rows, piece_rows, axis=0)
        full = lax.all_gather(piece, ('tp', 'ep'), axis=0, tiled=True)
        return full.reshape((tp_size,) + shard.shape)

    def layer(x_in, topk_idx, top_gate, g_attn, w_q, w_dkv, g_kv, w_ukv, w_o, g_ffn, w_gate, w_up, w_down, ws_gate, ws_up, ws_down):
        dims = model_dims(w_q, w_dkv, g_kv, w_ukv, w_o)
        kv_rank, rope_dim, heads, _, value_dim = dims
        expert_count = w_gate.shape[0]
        top_k = topk_idx.shape[-1]

        def device_work(x_loc, ids_loc, gate_loc, g_attn, w_q, w_dkv, g_kv, w_ukv, w_o, g_ffn, w_gate, w_up, w_down, ws_gate, ws_up, ws_down):
            bat, seq_loc, width = x_loc.shape
            toks = bat * seq_loc
            limit = 3 * (toks * top_k // expert_count)
            cap = -(-limit // 32) * 32
            z_idx = lax.axis_index('tp')
            ep_idx = lax.axis_index('ep')

            chunks = w_q.shape[0] // kv_rank
            q_cols = w_q.shape[1]
            packed = jnp.concatenate([w_ukv] + [w_q[part * kv_rank:(part + 1) * kv_rank] for part in range(chunks)], axis=1)
            packed = gather_weight(packed)
            full_o = gather_weight(w_o)
            weights = [w_gate, w_up, w_down] + [swap(w, core) for w in (w_gate, w_up, w_down)]

            x_rows = x_loc.reshape(toks, width)
            normed = rms_norm(x_rows, g_attn)
            latent = dot32(normed, w_dkv)
            cos_tab, sin_tab = rope_tables(z_idx * seq_loc + jnp.arange(seq_loc), rope_dim)
            c_kv = rms_norm(latent[:, :kv_rank], g_kv).reshape(bat, seq_loc, kv_rank)
            k_rope = rotate(latent[:, kv_rank:].reshape(bat, seq_loc, rope_dim), cos_tab, sin_tab)
            cache_loc = jnp.concatenate([c_kv, k_rope], axis=-1)
            caches = [cache_loc] + [from_plane(cache_loc, ahead) for ahead in range(1, tp_size)]

            masks = (0, flip_x, flip_y, flip_x | flip_y)
            slots = route_slots(ids_loc.reshape(toks, top_k), gate_loc.reshape(toks, top_k), expert_count, cap)
            slots = slots.reshape(2, tp_size, expert_count // tp_size, cap)
            plane_experts = jnp.concatenate([jnp.stack([2 * ((ep_idx ^ mask) ^ (j >> 1)) + (j & 1) for j in range(4)]) for mask in masks])
            homes = []
            for ahead in range(tp_size):
                mine = lax.dynamic_index_in_dim(slots, lax.rem(z_idx + tp_size - ahead, tp_size), axis=1, keepdims=False)
                homes.append((mine if ahead == 0 else from_plane(mine, ahead))[:, plane_experts])
            homes = jnp.stack(homes)
            toks_by_chip = homes[:, 0].astype(jnp.int32).reshape(tp_size, 4, 4, cap)
            wanted = jnp.stack([toks_by_chip[:, 0]] + [swap(toks_by_chip[:, which], masks[which]) for which in range(1, 4)], axis=2)
            small_all = (jnp.max(jnp.sum(wanted < toks, axis=3), axis=2) <= SMALL).astype(jnp.int32)
            home_cnt = jnp.sum(toks_by_chip < toks, axis=3).astype(jnp.int32).reshape(tp_size, 16)

            query = project(normed, packed, w_ukv.shape[1], q_cols)
            z_one = z_idx.astype(jnp.int32).reshape(1)
            heads_out = attend(query, caches, packed, z_one, cos_tab, sin_tab, dims)
            attn = dot32(heads_out, full_o.reshape(heads * value_dim, width)).astype(BF16)
            hidden = (x_rows.astype(F32) + attn.astype(F32)).astype(BF16)
            normed2 = rms_norm(hidden, g_ffn)

            half = toks // 2
            low, high = normed2[:half], normed2[half:]
            blocks = {}
            for ahead in (0, 2, 1, 3):
                lo = low if ahead == 0 else from_plane(low, ahead)
                hi = high if ahead == 0 else from_plane(high, ahead)
                lo_x, hi_y = swap(lo, flip_x), swap(hi, flip_y)
                lo_y, hi_x = swap(lo, flip_y), swap(hi, flip_x)
                lo_d, hi_d = swap(lo_x, flip_y), swap(hi_y, flip_x)
                blocks[ahead] = [lo, hi, lo_x, hi_x, lo_y, hi_y, lo_d, hi_d]

            shared_out = shared_experts(normed2, ws_gate, ws_up, ws_down)
            extra = {0: (), 1: (), 2: (), 3: ()}
            total = hidden.astype(F32) + shared_out
            for ahead in (2, 1, 3, 0):
                ids_wide = jnp.broadcast_to(wanted[ahead].reshape(16, cap)[:, :, None], (16, cap, 128))
                mine = experts(small_all[ahead], ids_wide, blocks[ahead], weights, cap)
                rows = [mine[0]] + [swap(mine[which], masks[which]) for which in range(1, 4)]
                part = combine(toks_by_chip[ahead].reshape(-1), homes[ahead, 1].reshape(-1), home_cnt[ahead], rows, extra[ahead], toks)
                if ahead == 2:
                    up = lax.ppermute(part, 'tp', [(i, i + 1) for i in range(tp_size // 2)])
                    down = lax.ppermute(part, 'tp', [(i, i - 1) for i in range(tp_size // 2, tp_size)])
                    extra[1], extra[3] = (up,), (down,)
                else:
                    total = total + (part if ahead == 0 else to_plane(part, ahead))
            y_loc = total.astype(BF16).reshape(bat, seq_loc, width)
            return y_loc, cache_loc

        return jax.shard_map(device_work, mesh=mesh, in_specs=in_specs, out_specs=(token_spec, token_spec), check_vma=False)(x_in, topk_idx, top_gate, g_attn, w_q, w_dkv, g_kv, w_ukv, w_o, g_ffn, w_gate, w_up, w_down, ws_gate, ws_up, ws_down)

    return layer
```

time: 3620 us -> 1750 us (0.48)
  the two profiles are of different devices: /device:TPU:25 before, /device:TPU:16 now
where the time goes in v1:
time: 1750 us
  waiting for transfers between devices  1020 us (58%)
  Pallas kernels  437 us (25%)
  starting transfers between devices  162 us (9%)
  local copies, waits for them, and re-layouts  63.3 us (4%)
  other arithmetic  32.8 us (2%)
    ppermute x42, waiting for transfers between devices, swap(): return lax.ppermute(values, 'ep', [(i, i ^ mask) for i in range(ep_size)])  644 us
    ppermute x12, waiting for transfers between devices, from_plane(): lax.ppermute(values, 'tp', [((i + ahead) % tp_size, i) for i in range(tp_...  375 us
    pallas_call x4, Pallas kernels, experts(): pl.pallas_call(functools.partial(experts_body, half), grid=(4,), in_specs...  234 us
    ppermute x42, starting transfers between devices, swap(): return lax.ppermute(values, 'ep', [(i, i ^ mask) for i in range(ep_size)])  136 us
    pallas_call x4, Pallas kernels, combine(): pl.pallas_call(combine_body, grid_spec=pltpu.PrefetchScalarGridSpec(num_s...  86.2 us
    pallas_call x1, Pallas kernels, attend(): pl.pallas_call(body, grid=(heads // 2, bat), in_specs=[pl.BlockSpec(memor...  60 us
    pallas_call x1, Pallas kernels, shared_experts(): pl.pallas_call(shared_body, grid=(inner // blk,), in_specs=[pl.BlockSpec(...  41.5 us
  transfers between devices with their start and end apart: 60, of which 22 were waited for; matrix products, arithmetic and copies ran while one was open for 4% of the time, Pallas kernels for 25%

profile of v1, /device:TPU:16, one launch (start us, length us, event | category | flops | bytes accessed | tf_op | source)
XLA Modules:
  0.0 1747.3 jit_solution(14884429240726790851)
XLA Ops:
  7.2 2.5 constant_dynamic-update-slice_fusion
  27.7 2.5 multiply_convert_fusion
  30.2 2.3 copy.114
  38.8 3.4 collective-permute-start.1
  44.1 11.5 select_reduce_fusion
  60.9 113.8 %collective-permute-done.3 = f32[2,16,224]{2,0,1:T(2,128)S(1)} collective-permute-done((f32[2,16,224]{2,0,1:T(2,128)S(1)}, f32[2,16,224]{2,0,1:T(2,128)S(1)}, u32[]{:S(2)}, u32[]{:S(2)}) %collective-permute-start.3) | collective-permute-done | bytes 28704 | tf_op jit(solution)/shard_map/ppermute | solution.py:370
  176.8 3.4 collective-permute-done.5
  193.5 14.7 project.1.q_ref
  208.3 60.0 %attend.1 = bf16[768,2048]{1,0:T(8,128)(2,1)} custom-call(s32[1]{0:T(128)} %bitcast.1.z_ref, bf16[4,768,768]{2,1,0:T(8,128)(2,1)} %project.1.q_ref, bf16[3,256,576]{2,1,0:T(8,128)(2,1)} %pad_maximum_fusion.c0, bf16[3,256,576]{2,1,0:T(8,128)(2,1)} %copy.119.c1, bf16[3,256,576]{2,1,0:T(8,128)(2,1)} %copy.120.c2, bf16[3,256,576]{2,1,0:T(8,128)(2,1)} %copy.121.c3, ...), custom_call_target="tpu_custom_call" | custom-call | flops 60000002048 | bytes 40000000 | tf_op jit(solution)/shard_map/attend/pallas_call | solution.py:109
  268.3 5.5 all-gather.5.cloned.1.call-done
  273.8 10.3 fusion
  294.3 97.5 %collective-permute-done.23.refs_0_ = bf16[384,2048]{1,0:T(8,128)(2,1)} collective-permute-done((bf16[384,2048]{1,0:T(8,128)(2,1)}, bf16[384,2048]{1,0:T(8,128)(2,1)}, u32[]{:S(2)}, u32[]{:S(2)}) %collective-permute-start.23) | collective-permute-done | bytes 1572896 | tf_op jit(solution)/shard_map/ppermute | solution.py:370
  393.3 32.2 %collective-permute-done.24.refs_1_ = bf16[384,2048]{1,0:T(8,128)(2,1)} collective-permute-done((bf16[384,2048]{1,0:T(8,128)(2,1)S(1)}, bf16[384,2048]{1,0:T(8,128)(2,1)}, u32[]{:S(2)}, u32[]{:S(2)}) %collective-permute-start.24) | collective-permute-done | bytes 1572896 | tf_op jit(solution)/shard_map/ppermute | solution.py:370
  427.0 66.0 %collective-permute-done.9.refs_0_ = bf16[384,2048]{1,0:T(8,128)(2,1)S(1)} collective-permute-done((bf16[384,2048]{1,0:T(8,128)(2,1)}, bf16[384,2048]{1,0:T(8,128)(2,1)S(1)}, u32[]{:S(2)}, u32[]{:S(2)}) %collective-permute-start.9) | collective-permute-done | bytes 1572896 | tf_op jit(solution)/shard_map/ppermute | solution.py:370
  493.0 4.7 collective-permute-start.37
  497.7 61.9 %collective-permute-done.10.refs_1_ = bf16[384,2048]{1,0:T(8,128)(2,1)S(1)} collective-permute-done((bf16[384,2048]{1,0:T(8,128)(2,1)S(1)}, bf16[384,2048]{1,0:T(8,128)(2,1)S(1)}, u32[]{:S(2)}, u32[]{:S(2)}) %collective-permute-start.10) | collective-permute-done | bytes 1572896 | tf_op jit(solution)/shard_map/ppermute | solution.py:370
  566.9 30.2 %collective-permute-done.26.refs_3_ = bf16[384,2048]{1,0:T(8,128)(2,1)} collective-permute-done((bf16[384,2048]{1,0:T(8,128)(2,1)}, bf16[384,2048]{1,0:T(8,128)(2,1)}, u32[]{:S(2)}, u32[]{:S(2)}) %collective-permute-start.26) | collective-permute-done | bytes 1572896 | tf_op jit(solution)/shard_map/ppermute | solution.py:367
  599.2 33.1 %collective-permute-done.29.refs_6_ = bf16[384,2048]{1,0:T(8,128)(2,1)} collective-permute-done((bf16[384,2048]{1,0:T(8,128)(2,1)}, bf16[384,2048]{1,0:T(8,128)(2,1)}, u32[]{:S(2)}, u32[]{:S(2)}) %collective-permute-start.29) | collective-permute-done | bytes 1572896 | tf_op jit(solution)/shard_map/ppermute | solution.py:367
  636.0 58.4 %experts.5 = (bf16[4,224,2048]{2,1,0:T(8,128)(2,1)}, bf16[4,224,2048]{2,1,0:T(8,128)(2,1)}, bf16[4,224,2048]{2,1,0:T(8,128)(2,1)}, bf16[4,224,2048]{2,1,0:T(8,128)(2,1)}) custom-call(s32[4]{0:T(128)} %get-tuple-element.57.small_ref, s32[16,224,128]{2,1,0:T(8,128)} %broadcast_in_dim.101.ids_ref, bf16[384,2048]{1,0:T(8,128)(2,1)} %collective-permute-done.23.refs_0_, ...), custom_call_target="tpu_custom_call" | custom-call | flops 60000002048 | bytes 100000000 | tf_op jit(solution)/shard_map/experts/pallas_call | solution.py:222
  694.4 16.3 collective-permute-start.31
  710.7 21.3 %collective-permute-done.11.refs_2_ = bf16[384,2048]{1,0:T(8,128)(2,1)} collective-permute-done((bf16[384,2048]{1,0:T(8,128)(2,1)}, bf16[384,2048]{1,0:T(8,128)(2,1)}, u32[]{:S(2)}, u32[]{:S(2)}) %collective-permute-start.11) | collective-permute-done | bytes 1572896 | tf_op jit(solution)/shard_map/ppermute | solution.py:367
  737.0 184.5 %collective-permute-done.38.refs_2_ = bf16[384,2048]{1,0:T(8,128)(2,1)} collective-permute-done((bf16[384,2048]{1,0:T(8,128)(2,1)}, bf16[384,2048]{1,0:T(8,128)(2,1)}, u32[]{:S(2)}, u32[]{:S(2)}) %collective-permute-start.38) | collective-permute-done | bytes 1572896 | tf_op jit(solution)/shard_map/ppermute | solution.py:367
  931.5 25.0 %collective-permute-done.15.refs_6_ = bf16[384,2048]{1,0:T(8,128)(2,1)S(1)} collective-permute-done((bf16[384,2048]{1,0:T(8,128)(2,1)}, bf16[384,2048]{1,0:T(8,128)(2,1)S(1)}, u32[]{:S(2)}, u32[]{:S(2)}) %collective-permute-start.15) | collective-permute-done | bytes 1572896 | tf_op jit(solution)/shard_map/ppermute | solution.py:367
  963.6 58.8 %experts.4 = (bf16[4,224,2048]{2,1,0:T(8,128)(2,1)}, bf16[4,224,2048]{2,1,0:T(8,128)(2,1)}, bf16[4,224,2048]{2,1,0:T(8,128)(2,1)}, bf16[4,224,2048]{2,1,0:T(8,128)(2,1)}) custom-call(s32[4]{0:T(128)} %get-tuple-element.54.small_ref, s32[16,224,128]{2,1,0:T(8,128)} %broadcast_in_dim.99.ids_ref, bf16[384,2048]{1,0:T(8,128)(2,1)} %copy-done.34, ...), custom_call_target="tpu_custom_call" | custom-call | flops 60000002048 | bytes 100000000 | tf_op jit(solution)/shard_map/experts/pallas_call | solution.py:222
  1026.6 20.3 %combine.4 = f32[768,2048]{1,0:T(8,128)} custom-call(s32[3584]{0:T(1024)S(1)} %copy-done, f32[3584]{0:T(1024)S(1)} %copy-done.1, s32[16]{0:T(128)S(1)} %copy-done.5, bf16[4,224,2048]{2,1,0:T(8,128)(2,1)S(1)} %copy-done.8, bf16[4,224,2048]{2,1,0:T(8,128)(2,1)} %collective-permute-done.31.r1, bf16[4,224,2048]{2,1,0:T(8,128)(2,1)} %collective-permute-done.32.r2, ...), custom_call_target="tpu_custom_call" | custom-call | flops 10000000000 | bytes 20000000 | tf_op jit(solution)/shard_map/combine/pallas_call | solution.py:293
  1047.0 16.2 collective-permute-start.20
  1063.1 15.6 collective-permute-start.21
  1081.5 4.6 collective-permute-start.47
  1087.8 58.4 %experts.6 = (bf16[4,224,2048]{2,1,0:T(8,128)(2,1)}, bf16[4,224,2048]{2,1,0:T(8,128)(2,1)}, bf16[4,224,2048]{2,1,0:T(8,128)(2,1)}, bf16[4,224,2048]{2,1,0:T(8,128)(2,1)}) custom-call(s32[4]{0:T(128)} %get-tuple-element.56.small_ref, s32[16,224,128]{2,1,0:T(8,128)} %broadcast_in_dim.103.ids_ref, bf16[384,2048]{1,0:T(8,128)(2,1)} %copy-done.33, ...), custom_call_target="tpu_custom_call" | custom-call | flops 60000002048 | bytes 100000000 | tf_op jit(solution)/shard_map/experts/pallas_call | solution.py:222
  1146.2 16.2 collective-permute-start.44
  1162.4 71.9 %collective-permute-done.21.r2 = bf16[4,224,2048]{2,1,0:T(8,128)(2,1)} collective-permute-done((bf16[4,224,2048]{2,1,0:T(8,128)(2,1)}, bf16[4,224,2048]{2,1,0:T(8,128)(2,1)}, u32[]{:S(2)}, u32[]{:S(2)}) %collective-permute-start.21) | collective-permute-done | bytes 3670048 | tf_op jit(solution)/shard_map/ppermute | solution.py:367
  1234.4 2.5 collective-permute-start.45
  1236.8 2.4 collective-permute-done.22.r3
  1243.3 57.6 %collective-permute-done.44.r1 = bf16[4,224,2048]{2,1,0:T(8,128)(2,1)} collective-permute-done((bf16[4,224,2048]{2,1,0:T(8,128)(2,1)}, bf16[4,224,2048]{2,1,0:T(8,128)(2,1)}, u32[]{:S(2)}, u32[]{:S(2)}) %collective-permute-start.44) | collective-permute-done | bytes 3670048 | tf_op jit(solution)/shard_map/ppermute | solution.py:367
  1303.0 89.5 %collective-permute-done.45.r2 = bf16[4,224,2048]{2,1,0:T(8,128)(2,1)} collective-permute-done((bf16[4,224,2048]{2,1,0:T(8,128)(2,1)}, bf16[4,224,2048]{2,1,0:T(8,128)(2,1)}, u32[]{:S(2)}, u32[]{:S(2)}) %collective-permute-start.45) | collective-permute-done | bytes 3670048 | tf_op jit(solution)/shard_map/ppermute | solution.py:367
  1392.5 2.5 collective-permute-start.51
  1399.6 22.6 %combine.5 = f32[768,2048]{1,0:T(8,128)} custom-call(s32[3584]{0:T(1024)S(1)} %reshape_squeeze.24.tok_ref, f32[3584]{0:T(1024)S(1)} %reshape_squeeze.25.gate_ref, s32[16]{0:T(128)S(1)} %copy-done.4, bf16[4,224,2048]{2,1,0:T(8,128)(2,1)S(1)} %copy-done.6, bf16[4,224,2048]{2,1,0:T(8,128)(2,1)} %collective-permute-done.20.r1, ...), custom_call_target="tpu_custom_call" | custom-call | flops 10000000000 | bytes 20000000 | tf_op jit(solution)/shard_map/combine/pallas_call | solution.py:293
  1422.3 22.5 %combine.6 = f32[768,2048]{1,0:T(8,128)} custom-call(s32[3584]{0:T(1024)S(1)} %reshape_squeeze.28.tok_ref, f32[3584]{0:T(1024)S(1)} %reshape_squeeze.29.gate_ref, s32[16]{0:T(128)S(1)} %copy-done.3, bf16[4,224,2048]{2,1,0:T(8,128)(2,1)S(1)} %copy-done.7, bf16[4,224,2048]{2,1,0:T(8,128)(2,1)} %collective-permute-done.44.r1, ...), custom_call_target="tpu_custom_call" | custom-call | flops 10000000000 | bytes 20000000 | tf_op jit(solution)/shard_map/combine/pallas_call | solution.py:293
  1445.3 15.0 collective-permute-done.53.refs_6_
  1460.4 2.3 broadcast_in_dim.105.ids_ref
  1462.7 58.5 %experts.7 = (bf16[4,224,2048]{2,1,0:T(8,128)(2,1)}, bf16[4,224,2048]{2,1,0:T(8,128)(2,1)}, bf16[4,224,2048]{2,1,0:T(8,128)(2,1)}, bf16[4,224,2048]{2,1,0:T(8,128)(2,1)}) custom-call(s32[4]{0:T(128)} %get-tuple-element.55.small_ref, s32[16,224,128]{2,1,0:T(8,128)} %broadcast_in_dim.105.ids_ref, bf16[384,2048]{1,0:T(8,128)(2,1)} %get-tuple-element.63.refs_0_, ...), custom_call_target="tpu_custom_call" | custom-call | flops 60000002048 | bytes 100000000 | tf_op jit(solution)/shard_map/experts/pallas_call | solution.py:222
  1521.2 16.4 collective-permute-start.55
  1537.7 14.3 collective-permute-start.56
  1555.1 41.5 %shared.1 = f32[768,2048]{1,0:T(8,128)} custom-call(bf16[768,2048]{1,0:T(8,128)(2,1)} %copy-done.11, bf16[2048,2816]{1,0:T(8,128)(2,1)} %gate_ref.1, bf16[2048,2816]{1,0:T(8,128)(2,1)} %up_ref.1, bf16[2816,2048]{1,0:T(8,128)(2,1)} %down_ref.1), custom_call_target="tpu_custom_call" | custom-call | flops 26575110144 | bytes 50000000 | tf_op jit(solution)/shard_map/shared/pallas_call | solution.py:327
  1596.6 21.6 %collective-permute-done.55.r1 = bf16[4,224,2048]{2,1,0:T(8,128)(2,1)} collective-permute-done((bf16[4,224,2048]{2,1,0:T(8,128)(2,1)}, bf16[4,224,2048]{2,1,0:T(8,128)(2,1)}, u32[]{:S(2)}, u32[]{:S(2)}) %collective-permute-start.55) | collective-permute-done | bytes 3670048 | tf_op jit(solution)/shard_map/ppermute | solution.py:367
  1618.2 88.0 %collective-permute-done.56.r2 = bf16[4,224,2048]{2,1,0:T(8,128)(2,1)} collective-permute-done((bf16[4,224,2048]{2,1,0:T(8,128)(2,1)}, bf16[4,224,2048]{2,1,0:T(8,128)(2,1)}, u32[]{:S(2)}, u32[]{:S(2)}) %collective-permute-start.56) | collective-permute-done | bytes 3670048 | tf_op jit(solution)/shard_map/ppermute | solution.py:367
  1710.0 20.8 %combine.7 = f32[768,2048]{1,0:T(8,128)} custom-call(s32[3584]{0:T(1024)S(1)} %reshape_squeeze.30.tok_ref, f32[3584]{0:T(1024)S(1)} %reshape_squeeze.31.gate_ref, s32[16]{0:T(128)S(1)} %copy-done.2, bf16[4,224,2048]{2,1,0:T(8,128)(2,1)S(1)} %copy-done.9, bf16[4,224,2048]{2,1,0:T(8,128)(2,1)} %collective-permute-done.55.r1, ...), custom_call_target="tpu_custom_call" | custom-call | flops 10000000000 | bytes 20000000 | tf_op jit(solution)/shard_map/combine/pallas_call | solution.py:293
  1730.9 9.3 fusion.6
  (258 shorter events, 121.8 us)
Async XLA Ops:
  7.2 186.4 %all-gather.3.cloned.1.call-start = ((), (), s32[]{:S(2)}) async-start(), calls=%async_computation | async-start | bytes 17301504 | tf_op jit(solution)/shard_map/all_gather | solution.py:378
  16.7 257.1 %all-gather.5.cloned.1.call-start = ((), (), s32[]{:S(2)}) async-start(), calls=%async_computation.1 | async-start | bytes 8650752 | tf_op jit(solution)/shard_map/all_gather | solution.py:378
  38.3 145.1 %collective-permute-start = (bf16[3,256,576]{1,2,0:T(8,128)(2,1)}, bf16[3,256,576]{1,2,0:T(8,128)(2,1)}, u32[]{:S(2)}, u32[]{:S(2)}) collective-permute-start(bf16[3,256,576]{1,2,0:T(8,128)(2,1)} %copy.116), channel_id=1, source_target_pairs={{8,0},{16,8},{24,16},{0,24},{9,1},{17,9},{25,17},{1,25},{10,2},{18... | collective-permute-start | bytes 2654216 | tf_op jit(solution)/shard_map/ppermute | solution.py:370
  38.8 147.4 %collective-permute-start.1 = (bf16[3,256,576]{1,2,0:T(8,128)(2,1)}, bf16[3,256,576]{1,2,0:T(8,128)(2,1)}, u32[]{:S(2)}, u32[]{:S(2)}) collective-permute-start(bf16[3,256,576]{1,2,0:T(8,128)(2,1)} %copy.116), channel_id=1, source_target_pairs={{16,0},{24,8},{0,16},{8,24},{17,1},{25,9},{1,17},{9,25},{18,2},{26... | collective-permute-start | bytes 2654216 | tf_op jit(solution)/shard_map/ppermute | solution.py:370
  42.2 147.5 %collective-permute-start.2 = (bf16[3,256,576]{1,2,0:T(8,128)(2,1)}, bf16[3,256,576]{1,2,0:T(8,128)(2,1)}, u32[]{:S(2)}, u32[]{:S(2)}) collective-permute-start(bf16[3,256,576]{1,2,0:T(8,128)(2,1)} %copy.116), channel_id=1, source_target_pairs={{24,0},{0,8},{8,16},{16,24},{25,1},{1,9},{9,17},{17,25},{26,2},{2,... | collective-permute-start | bytes 2654216 | tf_op jit(solution)/shard_map/ppermute | solution.py:370
  56.8 117.9 %collective-permute-start.3 = (f32[2,16,224]{2,0,1:T(2,128)S(1)}, f32[2,16,224]{2,0,1:T(2,128)S(1)}, u32[]{:S(2)}, u32[]{:S(2)}) collective-permute-start(f32[2,16,224]{2,0,1:T(2,128)S(1)} %bitcast.107), channel_id=1, source_target_pairs={{8,0},{16,8},{24,16},{0,24},{9,1},{17,9},{25,17},{1,25},{10,2},{18... | collective-permute-start | bytes 86024 | tf_op jit(solution)/shard_map/ppermute | solution.py:370
  58.8 117.3 %collective-permute-start.4 = (f32[2,16,224]{2,0,1:T(2,128)S(1)}, f32[2,16,224]{2,0,1:T(2,128)S(1)}, u32[]{:S(2)}, u32[]{:S(2)}) collective-permute-start(f32[2,16,224]{2,0,1:T(2,128)S(1)} %bitcast.106), channel_id=1, source_target_pairs={{16,0},{24,8},{0,16},{8,24},{17,1},{25,9},{1,17},{9,25},{18,2},{26... | collective-permute-start | bytes 86024 | tf_op jit(solution)/shard_map/ppermute | solution.py:370
  176.1 115.1 %collective-permute-start.17 = (bf16[2,2048,1408]{2,1,0:T(8,128)(2,1)}, bf16[2,2048,1408]{2,1,0:T(8,128)(2,1)}, u32[]{:S(2)}, u32[]{:S(2)}) collective-permute-start(bf16[2,2048,1408]{2,1,0:T(8,128)(2,1)} %refs_8_.7), channel_id=1, source_target_pairs={{0,1},{1,0},{2,3},{3,2},{4,5},{5,4},{6,7},{7,6},{8,9},{9,8},{10,11... | collective-permute-start | bytes 34603016 | tf_op jit(solution)/shard_map/ppermute | solution.py:367
  180.2 112.1 %collective-permute-start.18 = (bf16[2,2048,1408]{2,1,0:T(8,128)(2,1)}, bf16[2,2048,1408]{2,1,0:T(8,128)(2,1)}, u32[]{:S(2)}, u32[]{:S(2)}) collective-permute-start(bf16[2,2048,1408]{2,1,0:T(8,128)(2,1)} %refs_9_.7), channel_id=1, source_target_pairs={{0,1},{1,0},{2,3},{3,2},{4,5},{5,4},{6,7},{7,6},{8,9},{9,8},{10,11... | collective-permute-start | bytes 34603016 | tf_op jit(solution)/shard_map/ppermute | solution.py:367
  183.3 109.8 %collective-permute-start.19 = (bf16[2,1408,2048]{2,1,0:T(8,128)(2,1)}, bf16[2,1408,2048]{2,1,0:T(8,128)(2,1)}, u32[]{:S(2)}, u32[]{:S(2)}) collective-permute-start(bf16[2,1408,2048]{2,1,0:T(8,128)(2,1)} %refs_10_.7), channel_id=1, source_target_pairs={{0,1},{1,0},{2,3},{3,2},{4,5},{5,4},{6,7},{7,6},{8,9},{9,8},{10,11... | collective-permute-start | bytes 34603016 | tf_op jit(solution)/shard_map/ppermute | solution.py:367
  186.1 98.8 %collective-permute-start.6 = (s32[4,4,224]{2,0,1:T(4,128)S(1)}, s32[4,4,224]{2,0,1:T(4,128)S(1)}, u32[]{:S(2)}, u32[]{:S(2)}) collective-permute-start(s32[4,4,224]{2,0,1:T(4,128)S(1)} %get-tuple-element.77), channel_id=1, source_target_pairs={{0,2},{1,3},{2,0},{3,1},{4,6},{5,7},{6,4},{7,5},{8,10},{9,11},{10,... | collective-permute-start | bytes 43016 | tf_op jit(solution)/shard_map/ppermute | solution.py:367
  189.7 98.5 %collective-permute-start.7 = (s32[4,4,224]{2,0,1:T(4,128)S(1)}, s32[4,4,224]{2,0,1:T(4,128)S(1)}, u32[]{:S(2)}, u32[]{:S(2)}) collective-permute-start(s32[4,4,224]{2,0,1:T(4,128)S(1)} %get-tuple-element.76), channel_id=1, source_target_pairs={{0,4},{1,5},{2,6},{3,7},{4,0},{5,1},{6,2},{7,3},{8,12},{9,13},{10,... | collective-permute-start | bytes 43016 | tf_op jit(solution)/shard_map/ppermute | solution.py:367
  288.2 103.6 %collective-permute-start.23 = (bf16[384,2048]{1,0:T(8,128)(2,1)}, bf16[384,2048]{1,0:T(8,128)(2,1)}, u32[]{:S(2)}, u32[]{:S(2)}) collective-permute-start(bf16[384,2048]{1,0:T(8,128)(2,1)} %get-tuple-element.63.refs_0_), channel_id=1, source_target_pairs={{16,0},{24,8},{0,16},{8,24},{17,1},{25,9},{1,17},{9,25},{18,2},{26... | collective-permute-start | bytes 4718600 | tf_op jit(solution)/shard_map/ppermute | solution.py:370
  289.6 135.8 %collective-permute-start.24 = (bf16[384,2048]{1,0:T(8,128)(2,1)S(1)}, bf16[384,2048]{1,0:T(8,128)(2,1)}, u32[]{:S(2)}, u32[]{:S(2)}) collective-permute-start(bf16[384,2048]{1,0:T(8,128)(2,1)S(1)} %get-tuple-element.62.refs_1_), channel_id=1, source_target_pairs={{16,0},{24,8},{0,16},{8,24},{17,1},{25,9},{1,17},{9,25},{18,2},{26... | collective-permute-start | bytes 4718600 | tf_op jit(solution)/shard_map/ppermute | solution.py:370
  291.2 201.8 %collective-permute-start.9 = (bf16[384,2048]{1,0:T(8,128)(2,1)}, bf16[384,2048]{1,0:T(8,128)(2,1)S(1)}, u32[]{:S(2)}, u32[]{:S(2)}) collective-permute-start(bf16[384,2048]{1,0:T(8,128)(2,1)} %get-tuple-element.63.refs_0_), channel_id=1, source_target_pairs={{8,0},{16,8},{24,16},{0,24},{9,1},{17,9},{25,17},{1,25},{10,2},{18... | collective-permute-start | bytes 4718600 | tf_op jit(solution)/shard_map/ppermute | solution.py:370
  292.3 267.3 %collective-permute-start.10 = (bf16[384,2048]{1,0:T(8,128)(2,1)S(1)}, bf16[384,2048]{1,0:T(8,128)(2,1)S(1)}, u32[]{:S(2)}, u32[]{:S(2)}) collective-permute-start(bf16[384,2048]{1,0:T(8,128)(2,1)S(1)} %get-tuple-element.62.refs_1_), channel_id=1, source_target_pairs={{8,0},{16,8},{24,16},{0,24},{9,1},{17,9},{25,17},{1,25},{10,2},{18... | collective-permute-start | bytes 4718600 | tf_op jit(solution)/shard_map/ppermute | solution.py:370
  293.1 267.9 %collective-permute-start.36 = (bf16[384,2048]{1,0:T(8,128)(2,1)}, bf16[384,2048]{1,0:T(8,128)(2,1)S(1)}, u32[]{:S(2)}, u32[]{:S(2)}) collective-permute-start(bf16[384,2048]{1,0:T(8,128)(2,1)} %get-tuple-element.63.refs_0_), channel_id=1, source_target_pairs={{24,0},{0,8},{8,16},{16,24},{25,1},{1,9},{9,17},{17,25},{26,2},{2,... | collective-permute-start | bytes 4718600 | tf_op jit(solution)/shard_map/ppermute | solution.py:370
  391.9 169.8 %collective-permute-start.25 = (bf16[384,2048]{1,0:T(8,128)(2,1)}, bf16[384,2048]{1,0:T(8,128)(2,1)}, u32[]{:S(2)}, u32[]{:S(2)}) collective-permute-start(bf16[384,2048]{1,0:T(8,128)(2,1)} %collective-permute-done.23.refs_0_), channel_id=1, source_target_pairs={{0,2},{1,3},{2,0},{3,1},{4,6},{5,7},{6,4},{7,5},{8,10},{9,11},{10,... | collective-permute-start | bytes 4718600 | tf_op jit(solution)/shard_map/ppermute | solution.py:367
  425.5 137.6 %collective-permute-start.28 = (bf16[384,2048]{1,0:T(8,128)(2,1)}, bf16[384,2048]{1,0:T(8,128)(2,1)}, u32[]{:S(2)}, u32[]{:S(2)}) collective-permute-start(bf16[384,2048]{1,0:T(8,128)(2,1)} %collective-permute-done.24.refs_1_), channel_id=1, source_target_pairs={{0,4},{1,5},{2,6},{3,7},{4,0},{5,1},{6,2},{7,3},{8,12},{9,13},{10,... | collective-permute-start | bytes 4718600 | tf_op jit(solution)/shard_map/ppermute | solution.py:367
  565.5 128.8 %collective-permute-start.49 = (bf16[384,2048]{1,0:T(8,128)(2,1)}, bf16[384,2048]{1,0:T(8,128)(2,1)}, u32[]{:S(2)}, u32[]{:S(2)}) collective-permute-start(bf16[384,2048]{1,0:T(8,128)(2,1)} %get-tuple-element.63.refs_0_), channel_id=1, source_target_pairs={{0,2},{1,3},{2,0},{3,1},{4,6},{5,7},{6,4},{7,5},{8,10},{9,11},{10,... | collective-permute-start | bytes 4718600 | tf_op jit(solution)/shard_map/ppermute | solution.py:367
  597.2 136.3 %collective-permute-start.14 = (bf16[384,2048]{1,0:T(8,128)(2,1)}, bf16[384,2048]{1,0:T(8,128)(2,1)}, u32[]{:S(2)}, u32[]{:S(2)}) collective-permute-start(bf16[384,2048]{1,0:T(8,128)(2,1)} %copy-done.35), channel_id=1, source_target_pairs={{0,4},{1,5},{2,6},{3,7},{4,0},{5,1},{6,2},{7,3},{8,12},{9,13},{10,... | collective-permute-start | bytes 4718600 | tf_op jit(solution)/shard_map/ppermute | solution.py:367
  598.6 136.2 %collective-permute-start.12 = (bf16[384,2048]{1,0:T(8,128)(2,1)}, bf16[384,2048]{1,0:T(8,128)(2,1)}, u32[]{:S(2)}, u32[]{:S(2)}) collective-permute-start(bf16[384,2048]{1,0:T(8,128)(2,1)} %copy-done.35), channel_id=1, source_target_pairs={{0,2},{1,3},{2,0},{3,1},{4,6},{5,7},{6,4},{7,5},{8,10},{9,11},{10,... | collective-permute-start | bytes 4718600 | tf_op jit(solution)/shard_map/ppermute | solution.py:367
  632.3 99.7 %collective-permute-start.11 = (bf16[384,2048]{1,0:T(8,128)(2,1)}, bf16[384,2048]{1,0:T(8,128)(2,1)}, u32[]{:S(2)}, u32[]{:S(2)}) collective-permute-start(bf16[384,2048]{1,0:T(8,128)(2,1)} %copy-done.34), channel_id=1, source_target_pairs={{0,2},{1,3},{2,0},{3,1},{4,6},{5,7},{6,4},{7,5},{8,10},{9,11},{10,... | collective-permute-start | bytes 4718600 | tf_op jit(solution)/shard_map/ppermute | solution.py:367
  632.9 102.6 %collective-permute-start.13 = (bf16[384,2048]{1,0:T(8,128)(2,1)}, bf16[384,2048]{1,0:T(8,128)(2,1)}, u32[]{:S(2)}, u32[]{:S(2)}) collective-permute-start(bf16[384,2048]{1,0:T(8,128)(2,1)} %copy-done.34), channel_id=1, source_target_pairs={{0,4},{1,5},{2,6},{3,7},{4,0},{5,1},{6,2},{7,3},{8,12},{9,13},{10,... | collective-permute-start | bytes 4718600 | tf_op jit(solution)/shard_map/ppermute | solution.py:367
  694.4 264.2 %collective-permute-start.31 = (bf16[4,224,2048]{2,1,0:T(8,128)(2,1)}, bf16[4,224,2048]{2,1,0:T(8,128)(2,1)}, u32[]{:S(2)}, u32[]{:S(2)}) collective-permute-start(bf16[4,224,2048]{2,1,0:T(8,128)(2,1)} %get-tuple-element.23), channel_id=1, source_target_pairs={{0,2},{1,3},{2,0},{3,1},{4,6},{5,7},{6,4},{7,5},{8,10},{9,11},{10,... | collective-permute-start | bytes 11010056 | tf_op jit(solution)/shard_map/ppermute | solution.py:367
  732.0 228.0 %collective-permute-start.32 = (bf16[4,224,2048]{2,1,0:T(8,128)(2,1)}, bf16[4,224,2048]{2,1,0:T(8,128)(2,1)}, u32[]{:S(2)}, u32[]{:S(2)}) collective-permute-start(bf16[4,224,2048]{2,1,0:T(8,128)(2,1)} %get-tuple-element.24), channel_id=1, source_target_pairs={{0,4},{1,5},{2,6},{3,7},{4,0},{5,1},{6,2},{7,3},{8,12},{9,13},{10,... | collective-permute-start | bytes 11010056 | tf_op jit(solution)/shard_map/ppermute | solution.py:367
  733.5 227.1 %collective-permute-start.33 = (bf16[4,224,2048]{2,1,0:T(8,128)(2,1)}, bf16[4,224,2048]{2,1,0:T(8,128)(2,1)}, u32[]{:S(2)}, u32[]{:S(2)}) collective-permute-start(bf16[4,224,2048]{2,1,0:T(8,128)(2,1)} %get-tuple-element.25), channel_id=1, source_target_pairs={{0,6},{1,7},{2,4},{3,5},{4,2},{5,3},{6,0},{7,1},{8,14},{9,15},{10,... | collective-permute-start | bytes 11010056 | tf_op jit(solution)/shard_map/ppermute | solution.py:367
  734.9 186.6 %collective-permute-start.38 = (bf16[384,2048]{1,0:T(8,128)(2,1)}, bf16[384,2048]{1,0:T(8,128)(2,1)}, u32[]{:S(2)}, u32[]{:S(2)}) collective-permute-start(bf16[384,2048]{1,0:T(8,128)(2,1)} %copy-done.33), channel_id=1, source_target_pairs={{0,2},{1,3},{2,0},{3,1},{4,6},{5,7},{6,4},{7,5},{8,10},{9,11},{10,... | collective-permute-start | bytes 4718600 | tf_op jit(solution)/shard_map/ppermute | solution.py:367
  735.5 187.4 %collective-permute-start.41 = (bf16[384,2048]{1,0:T(8,128)(2,1)}, bf16[384,2048]{1,0:T(8,128)(2,1)}, u32[]{:S(2)}, u32[]{:S(2)}) collective-permute-start(bf16[384,2048]{1,0:T(8,128)(2,1)} %collective-permute-done.37.refs_1_), channel_id=1, source_target_pairs={{0,4},{1,5},{2,6},{3,7},{4,0},{5,1},{6,2},{7,3},{8,12},{9,13},{10,... | collective-permute-start | bytes 4718600 | tf_op jit(solution)/shard_map/ppermute | solution.py:367
  956.5 90.4 %collective-permute-start.52 = (bf16[384,2048]{1,0:T(8,128)(2,1)}, bf16[384,2048]{1,0:T(8,128)(2,1)}, u32[]{:S(2)}, u32[]{:S(2)}) collective-permute-start(bf16[384,2048]{1,0:T(8,128)(2,1)} %copy-done.18), channel_id=1, source_target_pairs={{0,4},{1,5},{2,6},{3,7},{4,0},{5,1},{6,2},{7,3},{8,12},{9,13},{10,... | collective-permute-start | bytes 4718600 | tf_op jit(solution)/shard_map/ppermute | solution.py:367
  958.0 105.1 %collective-permute-start.39 = (bf16[384,2048]{1,0:T(8,128)(2,1)}, bf16[384,2048]{1,0:T(8,128)(2,1)}, u32[]{:S(2)}, u32[]{:S(2)}) collective-permute-start(bf16[384,2048]{1,0:T(8,128)(2,1)} %collective-permute-done.37.refs_1_), channel_id=1, source_target_pairs={{0,2},{1,3},{2,0},{3,1},{4,6},{5,7},{6,4},{7,5},{8,10},{9,11},{10,... | collective-permute-start | bytes 4718600 | tf_op jit(solution)/shard_map/ppermute | solution.py:367
  958.6 120.1 %collective-permute-start.40 = (bf16[384,2048]{1,0:T(8,128)(2,1)}, bf16[384,2048]{1,0:T(8,128)(2,1)}, u32[]{:S(2)}, u32[]{:S(2)}) collective-permute-start(bf16[384,2048]{1,0:T(8,128)(2,1)} %copy-done.33), channel_id=1, source_target_pairs={{0,4},{1,5},{2,6},{3,7},{4,0},{5,1},{6,2},{7,3},{8,12},{9,13},{10,... | collective-permute-start | bytes 4718600 | tf_op jit(solution)/shard_map/ppermute | solution.py:367
  960.0 120.2 %collective-permute-start.42 = (bf16[384,2048]{1,0:T(8,128)(2,1)}, bf16[384,2048]{1,0:T(8,128)(2,1)}, u32[]{:S(2)}, u32[]{:S(2)}) collective-permute-start(bf16[384,2048]{1,0:T(8,128)(2,1)} %collective-permute-done.38.refs_2_), channel_id=1, source_target_pairs={{0,4},{1,5},{2,6},{3,7},{4,0},{5,1},{6,2},{7,3},{8,12},{9,13},{10,... | collective-permute-start | bytes 4718600 | tf_op jit(solution)/shard_map/ppermute | solution.py:367
  960.6 120.9 %collective-permute-start.43 = (bf16[384,2048]{1,0:T(8,128)(2,1)}, bf16[384,2048]{1,0:T(8,128)(2,1)}, u32[]{:S(2)}, u32[]{:S(2)}) collective-permute-start(bf16[384,2048]{1,0:T(8,128)(2,1)} %collective-permute-done.41.refs_5_), channel_id=1, source_target_pairs={{0,2},{1,3},{2,0},{3,1},{4,6},{5,7},{6,4},{7,5},{8,10},{9,11},{10,... | collective-permute-start | bytes 4718600 | tf_op jit(solution)/shard_map/ppermute | solution.py:367
  1047.0 99.2 %collective-permute-start.20 = (bf16[4,224,2048]{2,1,0:T(8,128)(2,1)}, bf16[4,224,2048]{2,1,0:T(8,128)(2,1)}, u32[]{:S(2)}, u32[]{:S(2)}) collective-permute-start(bf16[4,224,2048]{2,1,0:T(8,128)(2,1)} %get-tuple-element.19), channel_id=1, source_target_pairs={{0,2},{1,3},{2,0},{3,1},{4,6},{5,7},{6,4},{7,5},{8,10},{9,11},{10,... | collective-permute-start | bytes 11010056 | tf_op jit(solution)/shard_map/ppermute | solution.py:367
  1063.1 171.2 %collective-permute-start.21 = (bf16[4,224,2048]{2,1,0:T(8,128)(2,1)}, bf16[4,224,2048]{2,1,0:T(8,128)(2,1)}, u32[]{:S(2)}, u32[]{:S(2)}) collective-permute-start(bf16[4,224,2048]{2,1,0:T(8,128)(2,1)} %get-tuple-element.20), channel_id=1, source_target_pairs={{0,4},{1,5},{2,6},{3,7},{4,0},{5,1},{6,2},{7,3},{8,12},{9,13},{10,... | collective-permute-start | bytes 11010056 | tf_op jit(solution)/shard_map/ppermute | solution.py:367
  1078.7 160.5 %collective-permute-start.22 = (bf16[4,224,2048]{2,1,0:T(8,128)(2,1)}, bf16[4,224,2048]{2,1,0:T(8,128)(2,1)}, u32[]{:S(2)}, u32[]{:S(2)}) collective-permute-start(bf16[4,224,2048]{2,1,0:T(8,128)(2,1)} %get-tuple-element.21), channel_id=1, source_target_pairs={{0,6},{1,7},{2,4},{3,5},{4,2},{5,3},{6,0},{7,1},{8,14},{9,15},{10,... | collective-permute-start | bytes 11010056 | tf_op jit(solution)/shard_map/ppermute | solution.py:367
  1080.2 316.4 %collective-permute-start.34 = (f32[768,2048]{1,0:T(8,128)}, f32[768,2048]{1,0:T(8,128)}, u32[]{:S(2)}, u32[]{:S(2)}) collective-permute-start(f32[768,2048]{1,0:T(8,128)} %combine.4), channel_id=1, source_target_pairs={{0,8},{8,16},{1,9},{9,17},{2,10},{10,18},{3,11},{11,19},{4,12},{12... | collective-permute-start | bytes 18874376 | tf_op jit(solution)/shard_map/ppermute | solution.py:452
  1081.5 340.8 %collective-permute-start.47 = (f32[768,2048]{1,0:T(8,128)}, f32[768,2048]{1,0:T(8,128)}, u32[]{:S(2)}, u32[]{:S(2)}) collective-permute-start(f32[768,2048]{1,0:T(8,128)} %combine.4), channel_id=1, source_target_pairs={{16,8},{24,16},{17,9},{25,17},{18,10},{26,18},{19,11},{27,19},{20,... | collective-permute-start | bytes 18874376 | tf_op jit(solution)/shard_map/ppermute | solution.py:453
  1146.2 154.8 %collective-permute-start.44 = (bf16[4,224,2048]{2,1,0:T(8,128)(2,1)}, bf16[4,224,2048]{2,1,0:T(8,128)(2,1)}, u32[]{:S(2)}, u32[]{:S(2)}) collective-permute-start(bf16[4,224,2048]{2,1,0:T(8,128)(2,1)} %get-tuple-element.27), channel_id=1, source_target_pairs={{0,2},{1,3},{2,0},{3,1},{4,6},{5,7},{6,4},{7,5},{8,10},{9,11},{10,... | collective-permute-start | bytes 11010056 | tf_op jit(solution)/shard_map/ppermute | solution.py:367
  1234.4 158.2 %collective-permute-start.45 = (bf16[4,224,2048]{2,1,0:T(8,128)(2,1)}, bf16[4,224,2048]{2,1,0:T(8,128)(2,1)}, u32[]{:S(2)}, u32[]{:S(2)}) collective-permute-start(bf16[4,224,2048]{2,1,0:T(8,128)(2,1)} %get-tuple-element.28), channel_id=1, source_target_pairs={{0,4},{1,5},{2,6},{3,7},{4,0},{5,1},{6,2},{7,3},{8,12},{9,13},{10,... | collective-permute-start | bytes 11010056 | tf_op jit(solution)/shard_map/ppermute | solution.py:367
  1239.2 157.3 %collective-permute-start.46 = (bf16[4,224,2048]{2,1,0:T(8,128)(2,1)}, bf16[4,224,2048]{2,1,0:T(8,128)(2,1)}, u32[]{:S(2)}, u32[]{:S(2)}) collective-permute-start(bf16[4,224,2048]{2,1,0:T(8,128)(2,1)} %get-tuple-element.29), channel_id=1, source_target_pairs={{0,6},{1,7},{2,4},{3,5},{4,2},{5,3},{6,0},{7,1},{8,14},{9,15},{10,... | collective-permute-start | bytes 11010056 | tf_op jit(solution)/shard_map/ppermute | solution.py:367
  1301.0 143.8 %collective-permute-start.50 = (bf16[384,2048]{1,0:T(8,128)(2,1)}, bf16[384,2048]{1,0:T(8,128)(2,1)S(1)}, u32[]{:S(2)}, u32[]{:S(2)}) collective-permute-start(bf16[384,2048]{1,0:T(8,128)(2,1)} %copy-done.18), channel_id=1, source_target_pairs={{0,2},{1,3},{2,0},{3,1},{4,6},{5,7},{6,4},{7,5},{8,10},{9,11},{10,... | collective-permute-start | bytes 4718600 | tf_op jit(solution)/shard_map/ppermute | solution.py:367
  1422.2 308.6 %collective-permute-start.35 = (f32[768,2048]{1,0:T(8,128)}, f32[768,2048]{1,0:T(8,128)}, u32[]{:S(2)}, u32[]{:S(2)}) collective-permute-start(f32[768,2048]{1,0:T(8,128)} %combine.5), channel_id=1, source_target_pairs={{0,8},{8,16},{16,24},{24,0},{1,9},{9,17},{17,25},{25,1},{2,10},{10... | collective-permute-start | bytes 18874376 | tf_op jit(solution)/shard_map/ppermute | solution.py:373
  1444.7 286.1 %collective-permute-start.48 = (f32[768,2048]{1,0:T(8,128)}, f32[768,2048]{1,0:T(8,128)}, u32[]{:S(2)}, u32[]{:S(2)}) collective-permute-start(f32[768,2048]{1,0:T(8,128)} %combine.6), channel_id=1, source_target_pairs={{0,24},{8,0},{16,8},{24,16},{1,25},{9,1},{17,9},{25,17},{2,26},{10... | collective-permute-start | bytes 18874376 | tf_op jit(solution)/shard_map/ppermute | solution.py:373
  1521.2 97.0 %collective-permute-start.55 = (bf16[4,224,2048]{2,1,0:T(8,128)(2,1)}, bf16[4,224,2048]{2,1,0:T(8,128)(2,1)}, u32[]{:S(2)}, u32[]{:S(2)}) collective-permute-start(bf16[4,224,2048]{2,1,0:T(8,128)(2,1)} %get-tuple-element.31), channel_id=1, source_target_pairs={{0,2},{1,3},{2,0},{3,1},{4,6},{5,7},{6,4},{7,5},{8,10},{9,11},{10,... | collective-permute-start | bytes 11010056 | tf_op jit(solution)/shard_map/ppermute | solution.py:367
  1537.7 168.5 %collective-permute-start.56 = (bf16[4,224,2048]{2,1,0:T(8,128)(2,1)}, bf16[4,224,2048]{2,1,0:T(8,128)(2,1)}, u32[]{:S(2)}, u32[]{:S(2)}) collective-permute-start(bf16[4,224,2048]{2,1,0:T(8,128)(2,1)} %get-tuple-element.32), channel_id=1, source_target_pairs={{0,4},{1,5},{2,6},{3,7},{4,0},{5,1},{6,2},{7,3},{8,12},{9,13},{10,... | collective-permute-start | bytes 11010056 | tf_op jit(solution)/shard_map/ppermute | solution.py:367
  1552.0 156.0 %collective-permute-start.57 = (bf16[4,224,2048]{2,1,0:T(8,128)(2,1)}, bf16[4,224,2048]{2,1,0:T(8,128)(2,1)}, u32[]{:S(2)}, u32[]{:S(2)}) collective-permute-start(bf16[4,224,2048]{2,1,0:T(8,128)(2,1)} %get-tuple-element.33), channel_id=1, source_target_pairs={{0,6},{1,7},{2,4},{3,5},{4,2},{5,3},{6,0},{7,1},{8,14},{9,15},{10,... | collective-permute-start | bytes 11010056 | tf_op jit(solution)/shard_map/ppermute | solution.py:367
  (54 other events, 1512.0 us)
Sparse Core Ops, SparseCore 0:
  16.8 170.8 all-gather.2
  190.6 83.0 all-gather.4

commit v2 on v1

--- a/solution.py
+++ b/solution.py
@@ -45,83 +45,142 @@
     return jnp.dot(lhs, rhs, preferred_element_type=F32)
 
 
-def project_body(first, u_ref, w_ref, o_ref):
-    depth, cols = w_ref.shape[1], o_ref.shape[2]
-    total = jnp.zeros(o_ref.shape[1:], F32)
-    for part in range(u_ref.shape[1] // depth):
-        total = total + dot32(u_ref[:, part * depth:(part + 1) * depth], w_ref[0, :, first + part * cols:first + (part + 1) * cols])
-    o_ref[0] = total.astype(BF16)
-
-
-def project(rows, packed, first, cols):
-    toks, width = rows.shape
-    groups, depth, wide = packed.shape
+def latent_body(rank, x_ref, gain_ref, w_ref, gain_kv_ref, cos_ref, sin_ref, u_ref, cache_ref):
+    normed = rms_norm(x_ref[0], gain_ref[...])
+    u_ref[...] = normed
+    latent = dot32(normed, w_ref[...])
+    cache_ref[0, :, :rank] = rms_norm(latent[:, :rank], gain_kv_ref[...])
+    cache_ref[0, :, rank:] = rotate(latent[:, rank:], cos_ref[...], sin_ref[...])
+
+
+def latents(x_loc, g_attn, w_dkv, g_kv, cos_tab, sin_tab):
+    bat, seq, width = x_loc.shape
+    rank, wide = g_kv.shape[0], w_dkv.shape[1]
+    half_rope = (wide - rank) // 2
     return pl.pallas_call(
-        functools.partial(project_body, first),
-        grid=(groups,),
-        in_specs=[pl.BlockSpec((toks, width), lambda g: (0, 0)), pl.BlockSpec((1, depth, wide), lambda g: (g, 0, 0))],
-        out_specs=pl.BlockSpec((1, toks, cols), lambda g: (g, 0, 0)),
-        out_shape=jax.ShapeDtypeStruct((groups, toks, cols), BF16),
-        cost_estimate=pl.CostEstimate(flops=2 * toks * width * groups * cols, bytes_accessed=20_000_000, transcendentals=0),
-        name="project",
-    )(rows, packed)
-
-
-def attend_body(nope, rope, vdim, rank, z_ref, q_ref, c0, c1, c2, c3, w_ref, cos_ref, sin_ref, o_ref):
-    rows, blk = q_ref.shape[1], c0.shape[1]
+        functools.partial(latent_body, rank),
+        grid=(bat,),
+        in_specs=[
+            pl.BlockSpec((1, seq, width), lambda b: (b, 0, 0)),
+            pl.BlockSpec((1, width), lambda b: (0, 0)),
+            pl.BlockSpec((width, wide), lambda b: (0, 0)),
+            pl.BlockSpec((1, rank), lambda b: (0, 0)),
+            pl.BlockSpec((seq, half_rope), lambda b: (0, 0)),
+            pl.BlockSpec((seq, half_rope), lambda b: (0, 0)),
+        ],
+        out_specs=[pl.BlockSpec((seq, width), lambda b: (b, 0)), pl.BlockSpec((1, seq, wide), lambda b: (b, 0, 0))],
+        out_shape=[jax.ShapeDtypeStruct((bat * seq, width), BF16), jax.ShapeDtypeStruct((bat, seq, wide), BF16)],
+        cost_estimate=pl.CostEstimate(flops=2 * bat * seq * width * wide, bytes_accessed=12_000_000, transcendentals=0),
+        name="latents",
+    )(x_loc, g_attn.reshape(1, width), w_dkv, g_kv.reshape(1, rank), cos_tab, sin_tab)
+
+
+def group_body(dims, own, last, where_ref, u_ref, c0, c1, c2, c3, cos_ref, sin_ref, *refs):
+    rank, rope, _, nope, vdim = dims
+    weights, refs = (refs[:3], refs[3:]) if own else (refs[:2], refs[2:])
+    prev, refs = (None, refs) if own else (refs[0], refs[1:])
+    extras, refs = (refs[:2], refs[2:]) if last else ((), refs)
+    outs, (w_q, w_kv, w_o, sem) = refs[:-4], refs[-4:]
+    rows, blk = u_ref.shape[0], c0.shape[1]
     scale = (nope + rope) ** -0.5
+    z_idx, ep_idx = where_ref[0], where_ref[1]
+
+    @pl.when(pl.program_id(0) == 0)
+    def _():
+        copies = []
+        if own:
+            for index, dst in enumerate((w_q, w_kv, w_o)):
+                copies.append(pltpu.make_async_copy(weights[index], dst, sem.at[index]))
+        else:
+            q_rows, kv_rows = w_q.shape[0] // 8, w_kv.shape[0] // 8
+            cols = w_q.shape[1]
+            kv_cols, o_cols = w_kv.shape[1], w_o.shape[1]
+            spans = []
+            for part in range((kv_cols + o_cols) // cols):
+                lo, hi = part * cols, (part + 1) * cols
+                if lo < kv_cols:
+                    spans.append((part, 0, w_kv, lo, min(hi, kv_cols)))
+                if hi > kv_cols:
+                    spans.append((part, max(lo, kv_cols) - lo, w_o, max(lo, kv_cols) - kv_cols, hi - kv_cols))
+            for mask in range(8):
+                src = weights[mask & 1].at[mask >> 1]
+                block = ep_idx ^ mask
+                q_at = pl.ds(pl.multiple_of(block * q_rows, q_rows), q_rows)
+                kv_at = pl.ds(pl.multiple_of(block * kv_rows, kv_rows), kv_rows)
+                copies.append(pltpu.make_async_copy(src.at[:q_rows], w_q.at[q_at], sem.at[len(copies)]))
+                for part, first, dst, lo, hi in spans:
+                    top = q_rows + part * kv_rows
+                    copies.append(pltpu.make_async_copy(src.at[top:top + kv_rows, first:first + hi - lo], dst.at[kv_at, lo:hi], sem.at[len(copies)]))
+        for copy in copies:
+            copy.start()
+        for copy in copies:
+            copy.wait()
+
+    query = dot32(u_ref[...], w_q[...]).astype(BF16)
     cache = jnp.concatenate([c0[0], c1[0], c2[0], c3[0]], axis=0)
-    key_val = dot32(cache[:, :rank], w_ref[0]).astype(BF16)
+    key_val = dot32(cache[:, :rank], w_kv[...]).astype(BF16)
     k_rope = cache[:, rank:]
-    keys = 4 * blk
-    key_idx = lax.broadcasted_iota(jnp.int32, (1, keys), 1)
-    ahead = key_idx // blk
-    plane = z_ref[0] + ahead
-    plane = jnp.where(plane >= 4, plane - 4, plane)
-    key_pos = plane * blk + key_idx - ahead * blk
-    row_pos = z_ref[0] * blk + lax.broadcasted_iota(jnp.int32, (rows, keys), 0)
-    causal = row_pos >= key_pos
+    fold = scale * 1.4426950408889634
+    ahead = lax.broadcasted_iota(jnp.int32, (1, 3 * blk), 1) // blk + 1
+    hidden_keys = jnp.where(z_idx + ahead >= 4, 0.0, -jnp.inf)
+    causal = lax.broadcasted_iota(jnp.int32, (rows, blk), 0) >= lax.broadcasted_iota(jnp.int32, (rows, blk), 1)
     cos_tab, sin_tab = cos_ref[...], sin_ref[...]
     contract = (((1,), (1,)), ((), ()))
-    for head in range(2):
+    heads_out = []
+    for head in range(w_q.shape[1] // (nope + rope)):
         base = head * (nope + rope)
-        q_nope = q_ref[0, :, base:base + nope]
-        q_rope = rotate(q_ref[0, :, base + nope:base + nope + rope], cos_tab, sin_tab)
+        q_rope = rotate(query[:, base + nope:base + nope + rope], cos_tab, sin_tab)
+        q_head = jnp.concatenate([query[:, base:base + nope], q_rope], axis=1)
         start = head * (nope + vdim)
-        k_nope, value = key_val[:, start:start + nope], key_val[:, start + nope:start + nope + vdim]
-        scores = lax.dot_general(q_nope, k_nope, contract, preferred_element_type=F32)
-        scores = scores + lax.dot_general(q_rope, k_rope, contract, preferred_element_type=F32)
-        scores = jnp.where(causal, scores * scale, -jnp.inf)
-        unnorm = jnp.exp(scores - jnp.max(scores, axis=-1, keepdims=True))
-        prob = (unnorm * (1.0 / jnp.sum(unnorm, axis=-1, keepdims=True))).astype(BF16)
-        o_ref[:, head * vdim:(head + 1) * vdim] = dot32(prob, value).astype(BF16)
-
-
-def attend(query, caches, packed, z_one, cos_tab, sin_tab, dims):
-    rank, rope, heads, nope, vdim = dims
+        k_head = jnp.concatenate([key_val[:, start:start + nope], k_rope], axis=1)
+        value = key_val[:, start + nope:start + nope + vdim]
+        here = lax.dot_general(q_head, k_head[:blk], contract, preferred_element_type=F32)
+        here = jnp.where(causal, here, -jnp.inf)
+        there = lax.dot_general(q_head, k_head[blk:], contract, preferred_element_type=F32) + hidden_keys
+        top = jnp.maximum(jnp.max(here, axis=-1, keepdims=True), jnp.max(there, axis=-1, keepdims=True))
+        here, there = jnp.exp2((here - top) * fold), jnp.exp2((there - top) * fold)
+        inv = 1.0 / (jnp.sum(here, axis=-1, keepdims=True) + jnp.sum(there, axis=-1, keepdims=True))
+        head_out = dot32((here * inv).astype(BF16), value[:blk]) + dot32((there * inv).astype(BF16), value[blk:])
+        heads_out.append(head_out.astype(BF16))
+    total = dot32(jnp.concatenate(heads_out, axis=1), w_o[...])
+    if prev is not None:
+        total = total + prev[...]
+    if last:
+        hidden = (extras[0][0].astype(F32) + total.astype(BF16).astype(F32)).astype(BF16)
+        outs[0][...] = hidden
+        outs[1][...] = rms_norm(hidden, extras[1][...])
+    else:
+        outs[0][...] = total
+
+
+def attend_group(where, u_rows, caches, cos_tab, sin_tab, weights, prev, extras, dims, shapes):
+    _, rope, _, _, _ = dims
     bat, blk, wide = caches[0].shape
-    _, toks, qcols = query.shape
-    rows = toks // bat
-    pair = 2 * (nope + rope)
-    per = qcols // pair
-    kv_cols = 2 * (nope + vdim)
-    body = functools.partial(attend_body, nope, rope, vdim, rank)
+    width = u_rows.shape[1]
+    own, last = prev is None, bool(extras)
+    tok_spec = pl.BlockSpec((blk, width), lambda b: (b, 0))
+    table = pl.BlockSpec((blk, rope // 2), lambda b: (0, 0))
+    in_specs = [pl.BlockSpec(memory_space=pltpu.SMEM), tok_spec] + [pl.BlockSpec((1, blk, wide), lambda b: (b, 0, 0))] * 4 + [table, table]
+    in_specs += [pl.BlockSpec(memory_space=pl.ANY)] * len(weights)
+    args = [where, u_rows, *caches, cos_tab, sin_tab, *weights]
+    if not own:
+        in_specs.append(tok_spec)
+        args.append(prev)
+    if last:
+        in_specs += [pl.BlockSpec((1, blk, width), lambda b: (b, 0, 0)), pl.BlockSpec((1, width), lambda b: (0, 0))]
+        args += list(extras)
+    out = jax.ShapeDtypeStruct(u_rows.shape, BF16 if last else F32)
     return pl.pallas_call(
-        body,
-        grid=(heads // 2, bat),
-        in_specs=[
-            pl.BlockSpec(memory_space=pltpu.SMEM),
-            pl.BlockSpec((1, rows, pair), lambda h, b: (h // per, b, h % per)),
-        ] + [pl.BlockSpec((1, blk, wide), lambda h, b: (b, 0, 0))] * 4 + [
-            pl.BlockSpec((1, rank, kv_cols), lambda h, b: (h // per, 0, h % per)),
-            pl.BlockSpec((rows, rope // 2), lambda h, b: (0, 0)),
-            pl.BlockSpec((rows, rope // 2), lambda h, b: (0, 0)),
-        ],
-        out_specs=pl.BlockSpec((rows, 2 * vdim), lambda h, b: (b, h)),
-        out_shape=jax.ShapeDtypeStruct((toks, heads * vdim), BF16),
-        cost_estimate=pl.CostEstimate(flops=60_000_000_000, bytes_accessed=40_000_000, transcendentals=0),
+        functools.partial(group_body, dims, own, last),
+        grid=(bat,),
+        in_specs=in_specs,
+        out_specs=[tok_spec] * (2 if last else 1),
+        out_shape=[out] * (2 if last else 1),
+        scratch_shapes=[pltpu.VMEM(shape, BF16) for shape in shapes] + [pltpu.SemaphoreType.DMA((48,))],
+        compiler_params=pltpu.CompilerParams(vmem_limit_bytes=VMEM_MAX),
+        cost_estimate=pl.CostEstimate(flops=15_000_000_000, bytes_accessed=30_000_000, transcendentals=0),
         name="attend",
-    )(z_one, query, *caches, packed, cos_tab, sin_tab)
+    )(*args)
 
 
 def experts_body(half, small_ref, ids_ref, *refs):
@@ -256,17 +315,17 @@
     for which, src in enumerate((r0, r1, r2, r3)):
         @pl.when(step // 4 == which)
         def _():
-            @pl.loop(0, (cnt_ref[step] + 15) // 16)
+            @pl.loop(0, (cnt_ref[step] + 23) // 24)
             def _(group):
-                first = pl.multiple_of(group * 16, 16)
-                rows = src[0, pl.ds(first, 16), :].astype(F32)
+                first = pl.multiple_of(group * 24, 8)
+                rows = src[0, pl.ds(first, 24), :].astype(F32)
                 for blk in range(lanes):
-                    turn[pl.ds(blk, 16, stride=lanes), :] = rows[:, 128 * blk:128 * (blk + 1)]
+                    turn[pl.ds(blk, 24, stride=lanes), :] = rows[:, 128 * blk:128 * (blk + 1)]
                 base = step * cap + first
-                for part in range(2):
-                    spots = [pl.multiple_of(tok_ref[base + 8 * part + r] * lanes, lanes) for r in range(8)]
+                for part in range(0, 24, 8):
+                    spots = [pl.multiple_of(tok_ref[base + part + r] * lanes, lanes) for r in range(8)]
                     olds = [acc[pl.ds(spot, lanes), :] for spot in spots]
-                    news = [olds[r] + gate_ref[base + 8 * part + r] * turn[(8 * part + r) * lanes:(8 * part + r + 1) * lanes, :] for r in range(8)]
+                    news = [olds[r] + gate_ref[base + part + r] * turn[(part + r) * lanes:(part + r + 1) * lanes, :] for r in range(8)]
                     for r in range(8):
                         acc[pl.ds(spots[r], lanes), :] = news[r]
 
@@ -297,7 +356,7 @@
             grid=(16,),
             in_specs=[spec(which) for which in range(4)] + [whole] * len(extra),
             out_specs=whole,
-            scratch_shapes=[pltpu.VMEM(((toks + 1) * lanes, 128), F32), pltpu.VMEM((16 * lanes, 128), F32)],
+            scratch_shapes=[pltpu.VMEM(((toks + 1) * lanes, 128), F32), pltpu.VMEM((24 * lanes, 128), F32)],
         ),
         out_shape=jax.ShapeDtypeStruct((toks, width), F32),
         compiler_params=pltpu.CompilerParams(vmem_limit_bytes=48 * 2**20),
@@ -372,15 +431,15 @@
     def to_plane(values, ahead):
         return lax.ppermute(values, 'tp', [(i, (i + ahead) % tp_size) for i in range(tp_size)])
 
-    def gather_weight(shard):
-        piece_rows = shard.shape[0] // ep_size
-        piece = lax.dynamic_slice_in_dim(shard, lax.axis_index('ep') * piece_rows, piece_rows, axis=0)
-        full = lax.all_gather(piece, ('tp', 'ep'), axis=0, tiled=True)
-        return full.reshape((tp_size,) + shard.shape)
+    def relay(one, three):
+        half_tp = tp_size // 2
+        down = lax.ppermute(one, 'tp', [(i + 1, i) for i in range(half_tp)])
+        up = lax.ppermute(three, 'tp', [(i - 1, i) for i in range(half_tp, tp_size)])
+        return jnp.where(lax.axis_index('tp') < half_tp, down, up)
 
     def layer(x_in, topk_idx, top_gate, g_attn, w_q, w_dkv, g_kv, w_ukv, w_o, g_ffn, w_gate, w_up, w_down, ws_gate, ws_up, ws_down):
         dims = model_dims(w_q, w_dkv, g_kv, w_ukv, w_o)
-        kv_rank, rope_dim, heads, _, value_dim = dims
+        kv_rank, rope_dim, _, _, _ = dims
         expert_count = w_gate.shape[0]
         top_k = topk_idx.shape[-1]
 
@@ -388,25 +447,33 @@
             bat, seq_loc, width = x_loc.shape
             toks = bat * seq_loc
             limit = 3 * (toks * top_k // expert_count)
-            cap = -(-limit // 32) * 32
+            cap = -(-limit // 24) * 24
             z_idx = lax.axis_index('tp')
             ep_idx = lax.axis_index('ep')
 
-            chunks = w_q.shape[0] // kv_rank
+            q_rows, kv_rows = width // ep_size, kv_rank // ep_size
             q_cols = w_q.shape[1]
-            packed = jnp.concatenate([w_ukv] + [w_q[part * kv_rank:(part + 1) * kv_rank] for part in range(chunks)], axis=1)
-            packed = gather_weight(packed)
-            full_o = gather_weight(w_o)
+            rest = jnp.concatenate([lax.dynamic_slice_in_dim(w, ep_idx * kv_rows, kv_rows, axis=0) for w in (w_ukv, w_o)], axis=1)
+            parts = [lax.dynamic_slice_in_dim(w_q, ep_idx * q_rows, q_rows, axis=0)]
+            parts += [rest[:, first:first + q_cols] for first in range(0, rest.shape[1], q_cols)]
+            piece = jnp.concatenate(parts, axis=0)
+            quads, pairs, at_zs = {}, {}, {}
+            for ahead in (1, 3, 2):
+                at_z = relay(at_zs[1], at_zs[3]) if ahead == 2 else from_plane(piece, ahead)
+                at_zs[ahead] = at_z
+                at_x, at_y = swap(at_z, flip_x), swap(at_z, flip_y)
+                if ahead == 2:
+                    at_d = swap(at_z, flip_x | flip_y)
+                else:
+                    at_d = swap(at_y, flip_x) if ahead == 3 else swap(at_x, flip_y)
+                quads[ahead] = jnp.stack([at_z, at_x, at_y, at_d])
+                pairs[ahead] = swap(quads[ahead], core)
             weights = [w_gate, w_up, w_down] + [swap(w, core) for w in (w_gate, w_up, w_down)]
 
-            x_rows = x_loc.reshape(toks, width)
-            normed = rms_norm(x_rows, g_attn)
-            latent = dot32(normed, w_dkv)
             cos_tab, sin_tab = rope_tables(z_idx * seq_loc + jnp.arange(seq_loc), rope_dim)
-            c_kv = rms_norm(latent[:, :kv_rank], g_kv).reshape(bat, seq_loc, kv_rank)
-            k_rope = rotate(latent[:, kv_rank:].reshape(bat, seq_loc, rope_dim), cos_tab, sin_tab)
-            cache_loc = jnp.concatenate([c_kv, k_rope], axis=-1)
-            caches = [cache_loc] + [from_plane(cache_loc, ahead) for ahead in range(1, tp_size)]
+            u_rows, cache_loc = latents(x_loc, g_attn, w_dkv, g_kv, cos_tab, sin_tab)
+            cache_1, cache_3 = from_plane(cache_loc, 1), from_plane(cache_loc, 3)
+            caches = [cache_loc, cache_1, relay(cache_1, cache_3), cache_3]
 
             masks = (0, flip_x, flip_y, flip_x | flip_y)
             slots = route_slots(ids_loc.reshape(toks, top_k), gate_loc.reshape(toks, top_k), expert_count, cap)
@@ -422,38 +489,45 @@
             small_all = (jnp.max(jnp.sum(wanted < toks, axis=3), axis=2) <= SMALL).astype(jnp.int32)
             home_cnt = jnp.sum(toks_by_chip < toks, axis=3).astype(jnp.int32).reshape(tp_size, 16)
 
-            query = project(normed, packed, w_ukv.shape[1], q_cols)
-            z_one = z_idx.astype(jnp.int32).reshape(1)
-            heads_out = attend(query, caches, packed, z_one, cos_tab, sin_tab, dims)
-            attn = dot32(heads_out, full_o.reshape(heads * value_dim, width)).astype(BF16)
-            hidden = (x_rows.astype(F32) + attn.astype(F32)).astype(BF16)
-            normed2 = rms_norm(hidden, g_ffn)
+            where = jnp.stack([z_idx, ep_idx]).astype(jnp.int32)
+            shapes = (w_q.shape, w_ukv.shape, w_o.shape)
+            part = attend_group(where, u_rows, caches, cos_tab, sin_tab, (w_q, w_ukv, w_o), None, (), dims, shapes)[0]
+            for ahead in (1, 3):
+                part = attend_group(where, u_rows, caches, cos_tab, sin_tab, (quads[ahead], pairs[ahead]), part, (), dims, shapes)[0]
+            extras = (x_loc, g_ffn.reshape(1, width))
+            hidden, normed2 = attend_group(where, u_rows, caches, cos_tab, sin_tab, (quads[2], pairs[2]), part, extras, dims, shapes)
 
             half = toks // 2
             low, high = normed2[:half], normed2[half:]
             blocks = {}
-            for ahead in (0, 2, 1, 3):
+            for ahead in (0, 2, 1):
                 lo = low if ahead == 0 else from_plane(low, ahead)
                 hi = high if ahead == 0 else from_plane(high, ahead)
                 lo_x, hi_y = swap(lo, flip_x), swap(hi, flip_y)
                 lo_y, hi_x = swap(lo, flip_y), swap(hi, flip_x)
                 lo_d, hi_d = swap(lo_x, flip_y), swap(hi_y, flip_x)
                 blocks[ahead] = [lo, hi, lo_x, hi_x, lo_y, hi_y, lo_d, hi_d]
+            blocks[3] = [from_plane(block, 3) for block in blocks[0]]
 
             shared_out = shared_experts(normed2, ws_gate, ws_up, ws_down)
             extra = {0: (), 1: (), 2: (), 3: ()}
-            total = hidden.astype(F32) + shared_out
+            base, late = hidden.astype(F32) + shared_out, None
             for ahead in (2, 1, 3, 0):
                 ids_wide = jnp.broadcast_to(wanted[ahead].reshape(16, cap)[:, :, None], (16, cap, 128))
                 mine = experts(small_all[ahead], ids_wide, blocks[ahead], weights, cap)
                 rows = [mine[0]] + [swap(mine[which], masks[which]) for which in range(1, 4)]
+                if ahead == 0:
+                    extra[0] = (base,)
                 part = combine(toks_by_chip[ahead].reshape(-1), homes[ahead, 1].reshape(-1), home_cnt[ahead], rows, extra[ahead], toks)
                 if ahead == 2:
                     up = lax.ppermute(part, 'tp', [(i, i + 1) for i in range(tp_size // 2)])
                     down = lax.ppermute(part, 'tp', [(i, i - 1) for i in range(tp_size // 2, tp_size)])
                     extra[1], extra[3] = (up,), (down,)
-                else:
-                    total = total + (part if ahead == 0 else to_plane(part, ahead))
+                elif ahead == 1:
+                    base = base + to_plane(part, 1)
+                elif ahead == 3:
+                    late = to_plane(part, 3)
+            total = part + late
             y_loc = total.astype(BF16).reshape(bat, seq_loc, width)
             return y_loc, cache_loc
 

time: 1750 us -> 1600 us (0.914)
  waiting for transfers between devices: 1020 us -> 867 us
  Pallas kernels: 437 us -> 461 us
    ppermute x42 -> x48, waiting for transfers between devices: 644 us -> 487 us  [swap(): return lax.ppermute(values, 'ep', [(i, i ^ mask) for i in range(ep_size)])]
    ppermute x42 -> x48, starting transfers between devices: 136 us -> 103 us  [swap(): return lax.ppermute(values, 'ep', [(i, i ^ mask) for i in range(ep_size)])]
    ppermute x12 -> x19, starting transfers between devices: 18.9 us -> 46 us  [from_plane(): lax.ppermute(values, 'tp', [((i + ahead) % tp_size, i) for i in range(tp_...]
    pallas_call x2 -> x5, Pallas kernels: 74.7 us -> 101 us  [the longest x4 93.9 us: attend_group(): pl.pallas_call(functools.partial(group_body, dims, own, last), grid=(bat,...]
    ppermute x12 -> x19, waiting for transfers between devices: 375 us -> 374 us  [from_plane(): lax.ppermute(values, 'tp', [((i + ahead) % tp_size, i) for i in range(tp_...]
  transfers between devices with their start and end apart: 60 -> 75, of which waited for: 22 -> 38; matrix products, arithmetic and copies ran while one was open for 4% -> 5% of each run, Pallas kernels for 25% -> 27%
where the time goes in v2:
time: 1600 us
  waiting for transfers between devices  867 us (54%)
  Pallas kernels  461 us (29%)
  starting transfers between devices  167 us (10%)
  local copies, waits for them, and re-layouts  55.1 us (3%)
  other arithmetic  46.3 us (3%)
    ppermute x48, waiting for transfers between devices, swap(): return lax.ppermute(values, 'ep', [(i, i ^ mask) for i in range(ep_size)])  487 us
    ppermute x19, waiting for transfers between devices, from_plane(): lax.ppermute(values, 'tp', [((i + ahead) % tp_size, i) for i in range(tp_...  374 us
    pallas_call x4, Pallas kernels, experts(): pl.pallas_call(functools.partial(experts_body, half), grid=(4,), in_specs...  233 us
    ppermute x48, starting transfers between devices, swap(): return lax.ppermute(values, 'ep', [(i, i ^ mask) for i in range(ep_size)])  103 us
    pallas_call x4, Pallas kernels, attend_group(): pl.pallas_call(functools.partial(group_body, dims, own, last), grid=(bat,...  93.9 us
    pallas_call x4, Pallas kernels, combine(): pl.pallas_call(combine_body, grid_spec=pltpu.PrefetchScalarGridSpec(num_s...  85.9 us
    ppermute x19, starting transfers between devices, from_plane(): lax.ppermute(values, 'tp', [((i + ahead) % tp_size, i) for i in range(tp_...  46 us
    pallas_call x1, Pallas kernels, shared_experts(): pl.pallas_call(shared_body, grid=(inner // blk,), in_specs=[pl.BlockSpec(...  41.7 us
  transfers between devices with their start and end apart: 75, of which 38 were waited for; matrix products, arithmetic and copies ran while one was open for 5% of the time, Pallas kernels for 27%

profile of v2, /device:TPU:16, one launch (start us, length us, event | category | flops | bytes accessed | tf_op | source)
XLA Modules:
  0.0 1598.3 jit_solution(11774399153944503789)
XLA Ops:
  11.8 18.7 %collective-permute-done.10 = bf16[512,768]{1,0:T(8,128)(2,1)} collective-permute-done((bf16[512,768]{1,0:T(8,128)(2,1)}, bf16[512,768]{1,0:T(8,128)(2,1)}, u32[]{:S(2)}, u32[]{:S(2)}) %collective-permute-start.10) | collective-permute-done | bytes 786464 | tf_op jit(solution)/shard_map/ppermute | solution.py:429
  37.0 6.8 latents.1
  52.4 16.9 %collective-permute-done.6 = bf16[3,256,576]{1,2,0:T(8,128)(2,1)S(1)} collective-permute-done((bf16[3,256,576]{1,2,0:T(8,128)(2,1)S(1)}, bf16[3,256,576]{1,2,0:T(8,128)(2,1)S(1)}, u32[]{:S(2)}, u32[]{:S(2)}) %collective-permute-start.6) | collective-permute-done | bytes 884768 | tf_op jit(solution)/shard_map/ppermute | solution.py:429
  70.6 13.9 collective-permute-done.8
  93.2 6.4 collective-permute-done.24
  136.0 10.7 collective-permute-done.14
  146.6 12.9 collective-permute-done.16
  162.6 22.3 %attend.4.refs_2_ = f32[768,2048]{1,0:T(8,128)} custom-call(s32[2]{0:T(128)} %pad_add_fusion.1.where_ref, bf16[768,2048]{1,0:T(8,128)(2,1)} %get-tuple-element.22.u_ref, bf16[3,256,576]{2,1,0:T(8,128)(2,1)} %get-tuple-element.55.c0, bf16[3,256,576]{2,1,0:T(8,128)(2,1)} %copy.145.c1, bf16[3,256,576]{2,1,0:T(8,128)(2,1)} %broadcast_select_fusion.c2, ...), custom_call_target="tpu_custom_call" | custom-call | flops 15000000512 | bytes 30000000 | tf_op jit(solution)/shard_map/attend/pallas_call | solution.py:173
  184.9 23.4 %attend.5.refs_2_ = f32[768,2048]{1,0:T(8,128)} custom-call(s32[2]{0:T(128)} %pad_add_fusion.1.where_ref, bf16[768,2048]{1,0:T(8,128)(2,1)} %get-tuple-element.22.u_ref, bf16[3,256,576]{2,1,0:T(8,128)(2,1)} %get-tuple-element.55.c0, bf16[3,256,576]{2,1,0:T(8,128)(2,1)} %copy.145.c1, bf16[3,256,576]{2,1,0:T(8,128)(2,1)} %broadcast_select_fusion.c2, ...), custom_call_target="tpu_custom_call" | custom-call | flops 15000000512 | bytes 30000000 | tf_op jit(solution)/shard_map/attend/pallas_call | solution.py:173
  208.3 23.1 %attend.6.refs_2_ = f32[768,2048]{1,0:T(8,128)} custom-call(s32[2]{0:T(128)} %pad_add_fusion.1.where_ref, bf16[768,2048]{1,0:T(8,128)(2,1)} %get-tuple-element.22.u_ref, bf16[3,256,576]{2,1,0:T(8,128)(2,1)} %get-tuple-element.55.c0, bf16[3,256,576]{2,1,0:T(8,128)(2,1)} %copy.145.c1, bf16[3,256,576]{2,1,0:T(8,128)(2,1)} %broadcast_select_fusion.c2, ...), custom_call_target="tpu_custom_call" | custom-call | flops 15000000512 | bytes 30000000 | tf_op jit(solution)/shard_map/attend/pallas_call | solution.py:173
  231.4 25.2 %attend.7 = (bf16[768,2048]{1,0:T(8,128)(2,1)}, bf16[768,2048]{1,0:T(8,128)(2,1)}) custom-call(s32[2]{0:T(128)} %pad_add_fusion.1.where_ref, bf16[768,2048]{1,0:T(8,128)(2,1)} %get-tuple-element.22.u_ref, bf16[3,256,576]{2,1,0:T(8,128)(2,1)} %get-tuple-element.55.c0, bf16[3,256,576]{2,1,0:T(8,128)(2,1)} %copy.145.c1, ...), custom_call_target="tpu_custom_call" | custom-call | flops 15000000512 | bytes 30000000 | tf_op jit(solution)/shard_map/attend/pallas_call | solution.py:173
  260.6 9.8 select_reduce_fusion
  283.8 13.4 collective-permute-done.3
  306.6 33.7 %collective-permute-done.29.refs_5_ = bf16[384,2048]{1,0:T(8,128)(2,1)} collective-permute-done((bf16[384,2048]{1,0:T(8,128)(2,1)}, bf16[384,2048]{1,0:T(8,128)(2,1)}, u32[]{:S(2)}, u32[]{:S(2)}) %collective-permute-start.29) | collective-permute-done | bytes 1572896 | tf_op jit(solution)/shard_map/ppermute | solution.py:426
  340.8 32.4 %collective-permute-done.28.refs_4_ = bf16[384,2048]{1,0:T(8,128)(2,1)S(1)} collective-permute-done((bf16[384,2048]{1,0:T(8,128)(2,1)S(1)}, bf16[384,2048]{1,0:T(8,128)(2,1)S(1)}, u32[]{:S(2)}, u32[]{:S(2)}) %collective-permute-start.28) | collective-permute-done | bytes 1572896 | tf_op jit(solution)/shard_map/ppermute | solution.py:426
  377.6 83.6 %collective-permute-done.63.refs_1_ = bf16[384,2048]{1,0:T(8,128)(2,1)S(1)} collective-permute-done((bf16[384,2048]{1,0:T(8,128)(2,1)}, bf16[384,2048]{1,0:T(8,128)(2,1)S(1)}, u32[]{:S(2)}, u32[]{:S(2)}) %collective-permute-start.63) | collective-permute-done | bytes 1572896 | tf_op jit(solution)/shard_map/ppermute | solution.py:429
  461.3 45.6 %collective-permute-done.49.refs_0_ = bf16[384,2048]{1,0:T(8,128)(2,1)S(1)} collective-permute-done((bf16[384,2048]{1,0:T(8,128)(2,1)S(1)}, bf16[384,2048]{1,0:T(8,128)(2,1)S(1)}, u32[]{:S(2)}, u32[]{:S(2)}) %collective-permute-start.49) | collective-permute-done | bytes 1572896 | tf_op jit(solution)/shard_map/ppermute | solution.py:429
  506.8 21.2 %collective-permute-start.38 = (bf16[384,2048]{1,0:T(8,128)(2,1)S(1)}, bf16[384,2048]{1,0:T(8,128)(2,1)S(1)}, u32[]{:S(2)}, u32[]{:S(2)}) collective-permute-start(bf16[384,2048]{1,0:T(8,128)(2,1)S(1)} %get-tuple-element.71.refs_0_), channel_id=1, source_target_pairs={{8,0},{16,8},{24,16},{0,24},{9,1},{17,9},{25,17},{1,25},{10,2},{18... | collective-permute-start | bytes 4718600 | tf_op jit(solution)/shard_map/ppermute | solution.py:429
  528.1 12.6 collective-permute-done.50.refs_1_
  541.9 32.3 %collective-permute-done.38.refs_0_ = bf16[384,2048]{1,0:T(8,128)(2,1)S(1)} collective-permute-done((bf16[384,2048]{1,0:T(8,128)(2,1)S(1)}, bf16[384,2048]{1,0:T(8,128)(2,1)S(1)}, u32[]{:S(2)}, u32[]{:S(2)}) %collective-permute-start.38) | collective-permute-done | bytes 1572896 | tf_op jit(solution)/shard_map/ppermute | solution.py:429
  578.1 32.5 %collective-permute-done.54.refs_5_ = bf16[384,2048]{1,0:T(8,128)(2,1)} collective-permute-done((bf16[384,2048]{1,0:T(8,128)(2,1)S(1)}, bf16[384,2048]{1,0:T(8,128)(2,1)}, u32[]{:S(2)}, u32[]{:S(2)}) %collective-permute-start.54) | collective-permute-done | bytes 1572896 | tf_op jit(solution)/shard_map/ppermute | solution.py:426
  612.7 35.2 %collective-permute-done.53.refs_4_ = bf16[384,2048]{1,0:T(8,128)(2,1)S(1)} collective-permute-done((bf16[384,2048]{1,0:T(8,128)(2,1)S(1)}, bf16[384,2048]{1,0:T(8,128)(2,1)S(1)}, u32[]{:S(2)}, u32[]{:S(2)}) %collective-permute-start.53) | collective-permute-done | bytes 1572896 | tf_op jit(solution)/shard_map/ppermute | solution.py:426
  651.0 28.9 %collective-permute-done.55.refs_6_ = bf16[384,2048]{1,0:T(8,128)(2,1)} collective-permute-done((bf16[384,2048]{1,0:T(8,128)(2,1)S(1)}, bf16[384,2048]{1,0:T(8,128)(2,1)}, u32[]{:S(2)}, u32[]{:S(2)}) %collective-permute-start.55) | collective-permute-done | bytes 1572896 | tf_op jit(solution)/shard_map/ppermute | solution.py:426
  689.0 58.1 %experts.6 = (bf16[4,216,2048]{2,1,0:T(8,128)(2,1)}, bf16[4,216,2048]{2,1,0:T(8,128)(2,1)}, bf16[4,216,2048]{2,1,0:T(8,128)(2,1)}, bf16[4,216,2048]{2,1,0:T(8,128)(2,1)}) custom-call(s32[4]{0:T(128)} %get-tuple-element.63.small_ref, s32[16,216,128]{2,1,0:T(8,128)} %broadcast_in_dim.93.ids_ref, bf16[384,2048]{1,0:T(8,128)(2,1)} %copy-done.31, ...), custom_call_target="tpu_custom_call" | custom-call | flops 60000002048 | bytes 100000000 | tf_op jit(solution)/shard_map/experts/pallas_call | solution.py:281
  747.1 68.8 %collective-permute-done.39.refs_1_ = bf16[384,2048]{1,0:T(8,128)(2,1)} collective-permute-done((bf16[384,2048]{1,0:T(8,128)(2,1)}, bf16[384,2048]{1,0:T(8,128)(2,1)}, u32[]{:S(2)}, u32[]{:S(2)}) %collective-permute-start.39) | collective-permute-done | bytes 1572896 | tf_op jit(solution)/shard_map/ppermute | solution.py:429
  823.1 32.5 %collective-permute-done.66.refs_4_ = bf16[384,2048]{1,0:T(8,128)(2,1)S(1)} collective-permute-done((bf16[384,2048]{1,0:T(8,128)(2,1)}, bf16[384,2048]{1,0:T(8,128)(2,1)S(1)}, u32[]{:S(2)}, u32[]{:S(2)}) %collective-permute-start.66) | collective-permute-done | bytes 1572896 | tf_op jit(solution)/shard_map/ppermute | solution.py:429
  857.1 30.4 %collective-permute-done.67.refs_5_ = bf16[384,2048]{1,0:T(8,128)(2,1)S(1)} collective-permute-done((bf16[384,2048]{1,0:T(8,128)(2,1)}, bf16[384,2048]{1,0:T(8,128)(2,1)S(1)}, u32[]{:S(2)}, u32[]{:S(2)}) %collective-permute-start.67) | collective-permute-done | bytes 1572896 | tf_op jit(solution)/shard_map/ppermute | solution.py:429
  897.7 10.4 collective-permute-done.68.refs_6_
  908.1 11.8 collective-permute-start.42
  924.9 8.2 collective-permute-start.44
  936.2 58.2 %experts.7 = (bf16[4,216,2048]{2,1,0:T(8,128)(2,1)}, bf16[4,216,2048]{2,1,0:T(8,128)(2,1)}, bf16[4,216,2048]{2,1,0:T(8,128)(2,1)}, bf16[4,216,2048]{2,1,0:T(8,128)(2,1)}) custom-call(s32[4]{0:T(128)} %get-tuple-element.62.small_ref, s32[16,216,128]{2,1,0:T(8,128)} %broadcast_in_dim.95.ids_ref, bf16[384,2048]{1,0:T(8,128)(2,1)} %copy-done.29, ...), custom_call_target="tpu_custom_call" | custom-call | flops 60000002048 | bytes 100000000 | tf_op jit(solution)/shard_map/experts/pallas_call | solution.py:281
  994.4 66.0 %collective-permute-done.59.r3 = bf16[4,216,2048]{2,1,0:T(8,128)(2,1)} collective-permute-done((bf16[4,216,2048]{2,1,0:T(8,128)(2,1)}, bf16[4,216,2048]{2,1,0:T(8,128)(2,1)}, u32[]{:S(2)}, u32[]{:S(2)}) %collective-permute-start.59) | collective-permute-done | bytes 3538976 | tf_op jit(solution)/shard_map/ppermute | solution.py:426
  1064.5 19.9 %combine.4 = f32[768,2048]{1,0:T(8,128)} custom-call(s32[3456]{0:T(1024)S(1)} %copy-done, f32[3456]{0:T(1024)S(1)} %copy-done.1, s32[16]{0:T(128)S(1)} %copy-done.5, bf16[4,216,2048]{2,1,0:T(8,128)(2,1)S(1)} %copy-done.9, bf16[4,216,2048]{2,1,0:T(8,128)(2,1)} %collective-permute-done.57.r1, bf16[4,216,2048]{2,1,0:T(8,128)(2,1)} %collective-permute-done.58.r2, ...), custom_call_target="tpu_custom_call" | custom-call | flops 10000000000 | bytes 20000000 | tf_op jit(solution)/shard_map/combine/pallas_call | solution.py:352
  1093.0 58.1 %experts.5 = (bf16[4,216,2048]{2,1,0:T(8,128)(2,1)}, bf16[4,216,2048]{2,1,0:T(8,128)(2,1)}, bf16[4,216,2048]{2,1,0:T(8,128)(2,1)}, bf16[4,216,2048]{2,1,0:T(8,128)(2,1)}) custom-call(s32[4]{0:T(128)} %get-tuple-element.64.small_ref, s32[16,216,128]{2,1,0:T(8,128)} %broadcast_in_dim.91.ids_ref, bf16[384,2048]{1,0:T(8,128)(2,1)} %copy-done.28, ...), custom_call_target="tpu_custom_call" | custom-call | flops 60000002048 | bytes 100000000 | tf_op jit(solution)/shard_map/experts/pallas_call | solution.py:281
  1151.1 15.7 collective-permute-start.46
  1166.9 50.4 %collective-permute-done.71.r2 = bf16[4,216,2048]{2,1,0:T(8,128)(2,1)} collective-permute-done((bf16[4,216,2048]{2,1,0:T(8,128)(2,1)}, bf16[4,216,2048]{2,1,0:T(8,128)(2,1)}, u32[]{:S(2)}, u32[]{:S(2)}) %collective-permute-start.71) | collective-permute-done | bytes 3538976 | tf_op jit(solution)/shard_map/ppermute | solution.py:426
  1226.1 22.0 %combine.7 = f32[768,2048]{1,0:T(8,128)} custom-call(s32[3456]{0:T(1024)S(1)} %reshape_squeeze.30.tok_ref, f32[3456]{0:T(1024)S(1)} %reshape_squeeze.31.gate_ref, s32[16]{0:T(128)S(1)} %copy-done.4, bf16[4,216,2048]{2,1,0:T(8,128)(2,1)S(1)} %copy-done.6, bf16[4,216,2048]{2,1,0:T(8,128)(2,1)} %collective-permute-done.70.r1, ...), custom_call_target="tpu_custom_call" | custom-call | flops 10000000000 | bytes 20000000 | tf_op jit(solution)/shard_map/combine/pallas_call | solution.py:352
  1248.1 40.1 %collective-permute-done.46.r1 = bf16[4,216,2048]{2,1,0:T(8,128)(2,1)} collective-permute-done((bf16[4,216,2048]{2,1,0:T(8,128)(2,1)}, bf16[4,216,2048]{2,1,0:T(8,128)(2,1)}, u32[]{:S(2)}, u32[]{:S(2)}) %collective-permute-start.46) | collective-permute-done | bytes 3538976 | tf_op jit(solution)/shard_map/ppermute | solution.py:426
  1288.1 59.9 %collective-permute-done.47.r2 = bf16[4,216,2048]{2,1,0:T(8,128)(2,1)} collective-permute-done((bf16[4,216,2048]{2,1,0:T(8,128)(2,1)}, bf16[4,216,2048]{2,1,0:T(8,128)(2,1)}, u32[]{:S(2)}, u32[]{:S(2)}) %collective-permute-start.47) | collective-permute-done | bytes 3538976 | tf_op jit(solution)/shard_map/ppermute | solution.py:426
  1348.1 22.1 %combine.5 = f32[768,2048]{1,0:T(8,128)} custom-call(s32[3456]{0:T(1024)S(1)} %reshape_squeeze.26.tok_ref, f32[3456]{0:T(1024)S(1)} %reshape_squeeze.27.gate_ref, s32[16]{0:T(128)S(1)} %copy-done.3, bf16[4,216,2048]{2,1,0:T(8,128)(2,1)S(1)} %copy-done.7, bf16[4,216,2048]{2,1,0:T(8,128)(2,1)} %collective-permute-done.46.r1, ...), custom_call_target="tpu_custom_call" | custom-call | flops 10000000000 | bytes 20000000 | tf_op jit(solution)/shard_map/combine/pallas_call | solution.py:352
  1371.8 58.2 %experts.4 = (bf16[4,216,2048]{2,1,0:T(8,128)(2,1)}, bf16[4,216,2048]{2,1,0:T(8,128)(2,1)}, bf16[4,216,2048]{2,1,0:T(8,128)(2,1)}, bf16[4,216,2048]{2,1,0:T(8,128)(2,1)}) custom-call(s32[4]{0:T(128)} %get-tuple-element.65.small_ref, s32[16,216,128]{2,1,0:T(8,128)} %broadcast_in_dim.89.ids_ref, bf16[384,2048]{1,0:T(8,128)(2,1)} %copy-done.12, ...), custom_call_target="tpu_custom_call" | custom-call | flops 60000002048 | bytes 100000000 | tf_op jit(solution)/shard_map/experts/pallas_call | solution.py:281
  1430.0 16.0 %collective-permute-start.35 = (bf16[4,216,2048]{2,1,0:T(8,128)(2,1)}, bf16[4,216,2048]{2,1,0:T(8,128)(2,1)}, u32[]{:S(2)}, u32[]{:S(2)}) collective-permute-start(bf16[4,216,2048]{2,1,0:T(8,128)(2,1)} %get-tuple-element.26), channel_id=1, source_target_pairs={{0,2},{1,3},{2,0},{3,1},{4,6},{5,7},{6,4},{7,5},{8,10},{9,11},{10,... | collective-permute-start | bytes 10616840 | tf_op jit(solution)/shard_map/ppermute | solution.py:426
  1446.0 15.0 collective-permute-start.36
  1464.2 41.7 %shared.1 = f32[768,2048]{1,0:T(8,128)} custom-call(bf16[768,2048]{1,0:T(8,128)(2,1)} %get-tuple-element.24.rows_ref, bf16[2048,2816]{1,0:T(8,128)(2,1)} %gate_ref.1, bf16[2048,2816]{1,0:T(8,128)(2,1)} %up_ref.1, bf16[2816,2048]{1,0:T(8,128)(2,1)} %down_ref.1), custom_call_target="tpu_custom_call" | custom-call | flops 26575110144 | bytes 50000000 | tf_op jit(solution)/shard_map/shared/pallas_call | solution.py:386
  1505.9 9.8 add_add_fusion.rest_0_
  1516.0 51.0 %collective-permute-done.36.r2 = bf16[4,216,2048]{2,1,0:T(8,128)(2,1)} collective-permute-done((bf16[4,216,2048]{2,1,0:T(8,128)(2,1)}, bf16[4,216,2048]{2,1,0:T(8,128)(2,1)}, u32[]{:S(2)}, u32[]{:S(2)}) %collective-permute-start.36) | collective-permute-done | bytes 3538976 | tf_op jit(solution)/shard_map/ppermute | solution.py:426
  1568.8 22.0 %combine.6 = f32[768,2048]{1,0:T(8,128)} custom-call(s32[3456]{0:T(1024)S(1)} %reshape_squeeze.24.tok_ref, f32[3456]{0:T(1024)S(1)} %reshape_squeeze.25.gate_ref, s32[16]{0:T(128)S(1)} %copy-done.2, bf16[4,216,2048]{2,1,0:T(8,128)(2,1)S(1)} %copy-done.8, bf16[4,216,2048]{2,1,0:T(8,128)(2,1)} %collective-permute-done.35.r1, ...), custom_call_target="tpu_custom_call" | custom-call | flops 10000000000 | bytes 20000000 | tf_op jit(solution)/shard_map/combine/pallas_call | solution.py:352
  1590.8 7.3 add_convert_fusion
  (278 shorter events, 182.0 us)
Async XLA Ops:
  10.2 40.2 %collective-permute-start.12 = (bf16[512,768]{1,0:T(8,128)(2,1)}, bf16[512,768]{1,0:T(8,128)(2,1)}, u32[]{:S(2)}, u32[]{:S(2)}) collective-permute-start(bf16[512,768]{1,0:T(8,128)(2,1)} %dynamic-slice_dynamic-update-slice_fusion.1), channel_id=1, source_target_pairs={{24,0},{0,8},{8,16},{16,24},{25,1},{1,9},{9,17},{17,25},{26,2},{2,... | collective-permute-start | bytes 2359304 | tf_op jit(solution)/shard_map/ppermute | solution.py:429
  45.4 39.1 %collective-permute-start.8 = (bf16[3,256,576]{1,2,0:T(8,128)(2,1)S(1)}, bf16[3,256,576]{1,2,0:T(8,128)(2,1)S(1)}, u32[]{:S(2)}, u32[]{:S(2)}) collective-permute-start(bf16[3,256,576]{1,2,0:T(8,128)(2,1)S(1)} %copy.135), channel_id=1, source_target_pairs={{24,0},{0,8},{8,16},{16,24},{25,1},{1,9},{9,17},{17,25},{26,2},{2,... | collective-permute-start | bytes 2654216 | tf_op jit(solution)/shard_map/ppermute | solution.py:429
  48.9 40.7 %collective-permute-start.23 = (bf16[512,768]{1,0:T(8,128)(2,1)}, bf16[512,768]{1,0:T(8,128)(2,1)S(1)}, u32[]{:S(2)}, u32[]{:S(2)}) collective-permute-start(bf16[512,768]{1,0:T(8,128)(2,1)} %collective-permute-done.10), channel_id=1, source_target_pairs={{0,4},{1,5},{2,6},{3,7},{4,0},{5,1},{6,2},{7,3},{8,12},{9,13},{10,... | collective-permute-start | bytes 2359304 | tf_op jit(solution)/shard_map/ppermute | solution.py:426
  50.4 39.7 %collective-permute-start.19 = (bf16[512,768]{1,0:T(8,128)(2,1)}, bf16[512,768]{1,0:T(8,128)(2,1)}, u32[]{:S(2)}, u32[]{:S(2)}) collective-permute-start(bf16[512,768]{1,0:T(8,128)(2,1)} %collective-permute-done.12), channel_id=1, source_target_pairs={{0,4},{1,5},{2,6},{3,7},{4,0},{5,1},{6,2},{7,3},{8,12},{9,13},{10,... | collective-permute-start | bytes 2359304 | tf_op jit(solution)/shard_map/ppermute | solution.py:426
  50.9 48.7 %collective-permute-start.24 = (bf16[512,768]{1,0:T(8,128)(2,1)}, bf16[512,768]{1,0:T(8,128)(2,1)S(1)}, u32[]{:S(2)}, u32[]{:S(2)}) collective-permute-start(bf16[512,768]{1,0:T(8,128)(2,1)} %collective-permute-done.22), channel_id=1, source_target_pairs={{0,4},{1,5},{2,6},{3,7},{4,0},{5,1},{6,2},{7,3},{8,12},{9,13},{10,... | collective-permute-start | bytes 2359304 | tf_op jit(solution)/shard_map/ppermute | solution.py:426
  69.3 38.8 %collective-permute-start.11 = (bf16[512,768]{1,0:T(8,128)(2,1)}, bf16[512,768]{1,0:T(8,128)(2,1)S(1)}, u32[]{:S(2)}, u32[]{:S(2)}) collective-permute-start(bf16[512,768]{1,0:T(8,128)(2,1)} %collective-permute-done.10), channel_id=1, source_target_pairs={{8,0},{16,8},{9,1},{17,9},{10,2},{18,10},{11,3},{19,11},{12,4},{20... | collective-permute-start | bytes 2359304 | tf_op jit(solution)/shard_map/ppermute | solution.py:436
  109.6 75.4 %collective-permute-start.25 = (bf16[4,512,768]{2,1,0:T(8,128)(2,1)}, bf16[4,512,768]{2,1,0:T(8,128)(2,1)}, u32[]{:S(2)}, u32[]{:S(2)}) collective-permute-start(bf16[4,512,768]{2,1,0:T(8,128)(2,1)} %pad_maximum_fusion.2.refs_0_), channel_id=1, source_target_pairs={{0,1},{1,0},{2,3},{3,2},{4,5},{5,4},{6,7},{7,6},{8,9},{9,8},{10,11... | collective-permute-start | bytes 9437192 | tf_op jit(solution)/shard_map/ppermute | solution.py:426
  134.9 73.4 %collective-permute-start.21 = (bf16[4,512,768]{2,1,0:T(8,128)(2,1)}, bf16[4,512,768]{2,1,0:T(8,128)(2,1)}, u32[]{:S(2)}, u32[]{:S(2)}) collective-permute-start(bf16[4,512,768]{2,1,0:T(8,128)(2,1)} %pad_maximum_fusion.1.refs_0_), channel_id=1, source_target_pairs={{0,1},{1,0},{2,3},{3,2},{4,5},{5,4},{6,7},{7,6},{8,9},{9,8},{10,11... | collective-permute-start | bytes 9437192 | tf_op jit(solution)/shard_map/ppermute | solution.py:426
  162.6 68.8 %collective-permute-start.17 = (bf16[4,512,768]{2,1,0:T(8,128)(2,1)}, bf16[4,512,768]{2,1,0:T(8,128)(2,1)}, u32[]{:S(2)}, u32[]{:S(2)}) collective-permute-start(bf16[4,512,768]{2,1,0:T(8,128)(2,1)} %pad_maximum_fusion.refs_0_), channel_id=1, source_target_pairs={{0,1},{1,0},{2,3},{3,2},{4,5},{5,4},{6,7},{7,6},{8,9},{9,8},{10,11... | collective-permute-start | bytes 9437192 | tf_op jit(solution)/shard_map/ppermute | solution.py:426
  260.0 46.0 %collective-permute-start.26 = (bf16[384,2048]{1,0:T(8,128)(2,1)S(1)}, bf16[384,2048]{1,0:T(8,128)(2,1)}, u32[]{:S(2)}, u32[]{:S(2)}) collective-permute-start(bf16[384,2048]{1,0:T(8,128)(2,1)S(1)} %get-tuple-element.71.refs_0_), channel_id=1, source_target_pairs={{0,2},{1,3},{2,0},{3,1},{4,6},{5,7},{6,4},{7,5},{8,10},{9,11},{10,... | collective-permute-start | bytes 4718600 | tf_op jit(solution)/shard_map/ppermute | solution.py:426
  272.8 409.8 %collective-permute-start.32 = (bf16[2,2048,1408]{2,1,0:T(8,128)(2,1)}, bf16[2,2048,1408]{2,1,0:T(8,128)(2,1)}, u32[]{:S(2)}, u32[]{:S(2)}) collective-permute-start(bf16[2,2048,1408]{2,1,0:T(8,128)(2,1)} %refs_8_.7), channel_id=1, source_target_pairs={{0,1},{1,0},{2,3},{3,2},{4,5},{5,4},{6,7},{7,6},{8,9},{9,8},{10,11... | collective-permute-start | bytes 34603016 | tf_op jit(solution)/shard_map/ppermute | solution.py:426
  272.8 409.8 %collective-permute-start.33 = (bf16[2,2048,1408]{2,1,0:T(8,128)(2,1)}, bf16[2,2048,1408]{2,1,0:T(8,128)(2,1)}, u32[]{:S(2)}, u32[]{:S(2)}) collective-permute-start(bf16[2,2048,1408]{2,1,0:T(8,128)(2,1)} %refs_9_.7), channel_id=1, source_target_pairs={{0,1},{1,0},{2,3},{3,2},{4,5},{5,4},{6,7},{7,6},{8,9},{9,8},{10,11... | collective-permute-start | bytes 34603016 | tf_op jit(solution)/shard_map/ppermute | solution.py:426
  274.6 409.5 %collective-permute-start.34 = (bf16[2,1408,2048]{2,1,0:T(8,128)(2,1)}, bf16[2,1408,2048]{2,1,0:T(8,128)(2,1)}, u32[]{:S(2)}, u32[]{:S(2)}) collective-permute-start(bf16[2,1408,2048]{2,1,0:T(8,128)(2,1)} %refs_10_.7), channel_id=1, source_target_pairs={{0,1},{1,0},{2,3},{3,2},{4,5},{5,4},{6,7},{7,6},{8,9},{9,8},{10,11... | collective-permute-start | bytes 34603016 | tf_op jit(solution)/shard_map/ppermute | solution.py:426
  373.2 88.0 %collective-permute-start.63 = (bf16[384,2048]{1,0:T(8,128)(2,1)}, bf16[384,2048]{1,0:T(8,128)(2,1)S(1)}, u32[]{:S(2)}, u32[]{:S(2)}) collective-permute-start(bf16[384,2048]{1,0:T(8,128)(2,1)} %get-tuple-element.70.refs_1_), channel_id=1, source_target_pairs={{24,0},{0,8},{8,16},{16,24},{25,1},{1,9},{9,17},{17,25},{26,2},{2,... | collective-permute-start | bytes 4718600 | tf_op jit(solution)/shard_map/ppermute | solution.py:429
  373.7 133.1 %collective-permute-start.49 = (bf16[384,2048]{1,0:T(8,128)(2,1)S(1)}, bf16[384,2048]{1,0:T(8,128)(2,1)S(1)}, u32[]{:S(2)}, u32[]{:S(2)}) collective-permute-start(bf16[384,2048]{1,0:T(8,128)(2,1)S(1)} %get-tuple-element.71.refs_0_), channel_id=1, source_target_pairs={{16,0},{24,8},{0,16},{8,24},{17,1},{25,9},{1,17},{9,25},{18,2},{26... | collective-permute-start | bytes 4718600 | tf_op jit(solution)/shard_map/ppermute | solution.py:429
  461.2 79.4 %collective-permute-start.50 = (bf16[384,2048]{1,0:T(8,128)(2,1)}, bf16[384,2048]{1,0:T(8,128)(2,1)S(1)}, u32[]{:S(2)}, u32[]{:S(2)}) collective-permute-start(bf16[384,2048]{1,0:T(8,128)(2,1)} %get-tuple-element.70.refs_1_), channel_id=1, source_target_pairs={{16,0},{24,8},{0,16},{8,24},{17,1},{25,9},{1,17},{9,25},{18,2},{26... | collective-permute-start | bytes 4718600 | tf_op jit(solution)/shard_map/ppermute | solution.py:429
  506.8 67.4 %collective-permute-start.38 = (bf16[384,2048]{1,0:T(8,128)(2,1)S(1)}, bf16[384,2048]{1,0:T(8,128)(2,1)S(1)}, u32[]{:S(2)}, u32[]{:S(2)}) collective-permute-start(bf16[384,2048]{1,0:T(8,128)(2,1)S(1)} %get-tuple-element.71.refs_0_), channel_id=1, source_target_pairs={{8,0},{16,8},{24,16},{0,24},{9,1},{17,9},{25,17},{1,25},{10,2},{18... | collective-permute-start | bytes 4718600 | tf_op jit(solution)/shard_map/ppermute | solution.py:429
  610.6 37.3 %collective-permute-start.53 = (bf16[384,2048]{1,0:T(8,128)(2,1)S(1)}, bf16[384,2048]{1,0:T(8,128)(2,1)S(1)}, u32[]{:S(2)}, u32[]{:S(2)}) collective-permute-start(bf16[384,2048]{1,0:T(8,128)(2,1)S(1)} %collective-permute-done.49.refs_0_), channel_id=1, source_target_pairs={{0,4},{1,5},{2,6},{3,7},{4,0},{5,1},{6,2},{7,3},{8,12},{9,13},{10,... | collective-permute-start | bytes 4718600 | tf_op jit(solution)/shard_map/ppermute | solution.py:426
  612.3 67.6 %collective-permute-start.55 = (bf16[384,2048]{1,0:T(8,128)(2,1)S(1)}, bf16[384,2048]{1,0:T(8,128)(2,1)}, u32[]{:S(2)}, u32[]{:S(2)}) collective-permute-start(bf16[384,2048]{1,0:T(8,128)(2,1)S(1)} %collective-permute-done.51.refs_2_), channel_id=1, source_target_pairs={{0,4},{1,5},{2,6},{3,7},{4,0},{5,1},{6,2},{7,3},{8,12},{9,13},{10,... | collective-permute-start | bytes 4718600 | tf_op jit(solution)/shard_map/ppermute | solution.py:426
  679.9 136.0 %collective-permute-start.39 = (bf16[384,2048]{1,0:T(8,128)(2,1)}, bf16[384,2048]{1,0:T(8,128)(2,1)}, u32[]{:S(2)}, u32[]{:S(2)}) collective-permute-start(bf16[384,2048]{1,0:T(8,128)(2,1)} %get-tuple-element.70.refs_1_), channel_id=1, source_target_pairs={{8,0},{16,8},{24,16},{0,24},{9,1},{17,9},{25,17},{1,25},{10,2},{18... | collective-permute-start | bytes 4718600 | tf_op jit(solution)/shard_map/ppermute | solution.py:429
  682.4 134.8 %collective-permute-start.30 = (bf16[384,2048]{1,0:T(8,128)(2,1)}, bf16[384,2048]{1,0:T(8,128)(2,1)}, u32[]{:S(2)}, u32[]{:S(2)}) collective-permute-start(bf16[384,2048]{1,0:T(8,128)(2,1)} %collective-permute-done.26.refs_2_), channel_id=1, source_target_pairs={{0,4},{1,5},{2,6},{3,7},{4,0},{5,1},{6,2},{7,3},{8,12},{9,13},{10,... | collective-permute-start | bytes 4718600 | tf_op jit(solution)/shard_map/ppermute | solution.py:426
  682.7 135.0 %collective-permute-start.64 = (bf16[384,2048]{1,0:T(8,128)(2,1)}, bf16[384,2048]{1,0:T(8,128)(2,1)}, u32[]{:S(2)}, u32[]{:S(2)}) collective-permute-start(bf16[384,2048]{1,0:T(8,128)(2,1)} %collective-permute-done.26.refs_2_), channel_id=1, source_target_pairs={{24,0},{0,8},{8,16},{16,24},{25,1},{1,9},{9,17},{17,25},{26,2},{2,... | collective-permute-start | bytes 4718600 | tf_op jit(solution)/shard_map/ppermute | solution.py:429
  682.7 135.0 %collective-permute-start.31 = (bf16[384,2048]{1,0:T(8,128)(2,1)}, bf16[384,2048]{1,0:T(8,128)(2,1)}, u32[]{:S(2)}, u32[]{:S(2)}) collective-permute-start(bf16[384,2048]{1,0:T(8,128)(2,1)} %collective-permute-done.29.refs_5_), channel_id=1, source_target_pairs={{0,2},{1,3},{2,0},{3,1},{4,6},{5,7},{6,4},{7,5},{8,10},{9,11},{10,... | collective-permute-start | bytes 4718600 | tf_op jit(solution)/shard_map/ppermute | solution.py:426
  684.2 138.3 %collective-permute-start.65 = (bf16[384,2048]{1,0:T(8,128)(2,1)}, bf16[384,2048]{1,0:T(8,128)(2,1)}, u32[]{:S(2)}, u32[]{:S(2)}) collective-permute-start(bf16[384,2048]{1,0:T(8,128)(2,1)} %collective-permute-done.27.refs_3_), channel_id=1, source_target_pairs={{24,0},{0,8},{8,16},{16,24},{25,1},{1,9},{9,17},{17,25},{26,2},{2,... | collective-permute-start | bytes 4718600 | tf_op jit(solution)/shard_map/ppermute | solution.py:429
  815.9 117.2 %collective-permute-start.57 = (bf16[4,216,2048]{2,1,0:T(8,128)(2,1)}, bf16[4,216,2048]{2,1,0:T(8,128)(2,1)}, u32[]{:S(2)}, u32[]{:S(2)}) collective-permute-start(bf16[4,216,2048]{2,1,0:T(8,128)(2,1)} %get-tuple-element.35), channel_id=1, source_target_pairs={{0,2},{1,3},{2,0},{3,1},{4,6},{5,7},{6,4},{7,5},{8,10},{9,11},{10,... | collective-permute-start | bytes 10616840 | tf_op jit(solution)/shard_map/ppermute | solution.py:426
  817.1 116.0 %collective-permute-start.58 = (bf16[4,216,2048]{2,1,0:T(8,128)(2,1)}, bf16[4,216,2048]{2,1,0:T(8,128)(2,1)}, u32[]{:S(2)}, u32[]{:S(2)}) collective-permute-start(bf16[4,216,2048]{2,1,0:T(8,128)(2,1)} %get-tuple-element.36), channel_id=1, source_target_pairs={{0,4},{1,5},{2,6},{3,7},{4,0},{5,1},{6,2},{7,3},{8,12},{9,13},{10,... | collective-permute-start | bytes 10616840 | tf_op jit(solution)/shard_map/ppermute | solution.py:426
  817.7 37.9 %collective-permute-start.66 = (bf16[384,2048]{1,0:T(8,128)(2,1)}, bf16[384,2048]{1,0:T(8,128)(2,1)S(1)}, u32[]{:S(2)}, u32[]{:S(2)}) collective-permute-start(bf16[384,2048]{1,0:T(8,128)(2,1)} %copy-done.27), channel_id=1, source_target_pairs={{24,0},{0,8},{8,16},{16,24},{25,1},{1,9},{9,17},{17,25},{26,2},{2,... | collective-permute-start | bytes 4718600 | tf_op jit(solution)/shard_map/ppermute | solution.py:429
  817.7 69.8 %collective-permute-start.67 = (bf16[384,2048]{1,0:T(8,128)(2,1)}, bf16[384,2048]{1,0:T(8,128)(2,1)S(1)}, u32[]{:S(2)}, u32[]{:S(2)}) collective-permute-start(bf16[384,2048]{1,0:T(8,128)(2,1)} %collective-permute-done.29.refs_5_), channel_id=1, source_target_pairs={{24,0},{0,8},{8,16},{16,24},{25,1},{1,9},{9,17},{17,25},{26,2},{2,... | collective-permute-start | bytes 4718600 | tf_op jit(solution)/shard_map/ppermute | solution.py:429
  822.5 65.0 %collective-permute-start.40 = (bf16[384,2048]{1,0:T(8,128)(2,1)}, bf16[384,2048]{1,0:T(8,128)(2,1)}, u32[]{:S(2)}, u32[]{:S(2)}) collective-permute-start(bf16[384,2048]{1,0:T(8,128)(2,1)} %copy-done.28), channel_id=1, source_target_pairs={{0,2},{1,3},{2,0},{3,1},{4,6},{5,7},{6,4},{7,5},{8,10},{9,11},{10,... | collective-permute-start | bytes 4718600 | tf_op jit(solution)/shard_map/ppermute | solution.py:426
  855.6 40.9 %collective-permute-start.43 = (bf16[384,2048]{1,0:T(8,128)(2,1)}, bf16[384,2048]{1,0:T(8,128)(2,1)}, u32[]{:S(2)}, u32[]{:S(2)}) collective-permute-start(bf16[384,2048]{1,0:T(8,128)(2,1)} %collective-permute-done.39.refs_1_), channel_id=1, source_target_pairs={{0,4},{1,5},{2,6},{3,7},{4,0},{5,1},{6,2},{7,3},{8,12},{9,13},{10,... | collective-permute-start | bytes 4718600 | tf_op jit(solution)/shard_map/ppermute | solution.py:426
  896.5 187.8 %collective-permute-start.41 = (bf16[384,2048]{1,0:T(8,128)(2,1)}, bf16[384,2048]{1,0:T(8,128)(2,1)}, u32[]{:S(2)}, u32[]{:S(2)}) collective-permute-start(bf16[384,2048]{1,0:T(8,128)(2,1)} %collective-permute-done.39.refs_1_), channel_id=1, source_target_pairs={{0,2},{1,3},{2,0},{3,1},{4,6},{5,7},{6,4},{7,5},{8,10},{9,11},{10,... | collective-permute-start | bytes 4718600 | tf_op jit(solution)/shard_map/ppermute | solution.py:426
  908.1 176.4 %collective-permute-start.42 = (bf16[384,2048]{1,0:T(8,128)(2,1)}, bf16[384,2048]{1,0:T(8,128)(2,1)}, u32[]{:S(2)}, u32[]{:S(2)}) collective-permute-start(bf16[384,2048]{1,0:T(8,128)(2,1)} %copy-done.28), channel_id=1, source_target_pairs={{0,4},{1,5},{2,6},{3,7},{4,0},{5,1},{6,2},{7,3},{8,12},{9,13},{10,... | collective-permute-start | bytes 4718600 | tf_op jit(solution)/shard_map/ppermute | solution.py:426
  924.9 162.9 %collective-permute-start.44 = (bf16[384,2048]{1,0:T(8,128)(2,1)}, bf16[384,2048]{1,0:T(8,128)(2,1)}, u32[]{:S(2)}, u32[]{:S(2)}) collective-permute-start(bf16[384,2048]{1,0:T(8,128)(2,1)} %collective-permute-done.40.refs_2_), channel_id=1, source_target_pairs={{0,4},{1,5},{2,6},{3,7},{4,0},{5,1},{6,2},{7,3},{8,12},{9,13},{10,... | collective-permute-start | bytes 4718600 | tf_op jit(solution)/shard_map/ppermute | solution.py:426
  933.2 156.6 %collective-permute-start.45 = (bf16[384,2048]{1,0:T(8,128)(2,1)}, bf16[384,2048]{1,0:T(8,128)(2,1)}, u32[]{:S(2)}, u32[]{:S(2)}) collective-permute-start(bf16[384,2048]{1,0:T(8,128)(2,1)} %collective-permute-done.43.refs_5_), channel_id=1, source_target_pairs={{0,2},{1,3},{2,0},{3,1},{4,6},{5,7},{6,4},{7,5},{8,10},{9,11},{10,... | collective-permute-start | bytes 4718600 | tf_op jit(solution)/shard_map/ppermute | solution.py:426
  933.2 127.2 %collective-permute-start.59 = (bf16[4,216,2048]{2,1,0:T(8,128)(2,1)}, bf16[4,216,2048]{2,1,0:T(8,128)(2,1)}, u32[]{:S(2)}, u32[]{:S(2)}) collective-permute-start(bf16[4,216,2048]{2,1,0:T(8,128)(2,1)} %get-tuple-element.37), channel_id=1, source_target_pairs={{0,6},{1,7},{2,4},{3,5},{4,2},{5,3},{6,0},{7,1},{8,14},{9,15},{10,... | collective-permute-start | bytes 10616840 | tf_op jit(solution)/shard_map/ppermute | solution.py:426
  1060.4 90.8 %collective-permute-start.70 = (bf16[4,216,2048]{2,1,0:T(8,128)(2,1)}, bf16[4,216,2048]{2,1,0:T(8,128)(2,1)}, u32[]{:S(2)}, u32[]{:S(2)}) collective-permute-start(bf16[4,216,2048]{2,1,0:T(8,128)(2,1)} %get-tuple-element.39), channel_id=1, source_target_pairs={{0,2},{1,3},{2,0},{3,1},{4,6},{5,7},{6,4},{7,5},{8,10},{9,11},{10,... | collective-permute-start | bytes 10616840 | tf_op jit(solution)/shard_map/ppermute | solution.py:426
  1084.3 133.0 %collective-permute-start.71 = (bf16[4,216,2048]{2,1,0:T(8,128)(2,1)}, bf16[4,216,2048]{2,1,0:T(8,128)(2,1)}, u32[]{:S(2)}, u32[]{:S(2)}) collective-permute-start(bf16[4,216,2048]{2,1,0:T(8,128)(2,1)} %get-tuple-element.40), channel_id=1, source_target_pairs={{0,4},{1,5},{2,6},{3,7},{4,0},{5,1},{6,2},{7,3},{8,12},{9,13},{10,... | collective-permute-start | bytes 10616840 | tf_op jit(solution)/shard_map/ppermute | solution.py:426
  1084.5 132.8 %collective-permute-start.72 = (bf16[4,216,2048]{2,1,0:T(8,128)(2,1)}, bf16[4,216,2048]{2,1,0:T(8,128)(2,1)}, u32[]{:S(2)}, u32[]{:S(2)}) collective-permute-start(bf16[4,216,2048]{2,1,0:T(8,128)(2,1)} %get-tuple-element.41), channel_id=1, source_target_pairs={{0,6},{1,7},{2,4},{3,5},{4,2},{5,3},{6,0},{7,1},{8,14},{9,15},{10,... | collective-permute-start | bytes 10616840 | tf_op jit(solution)/shard_map/ppermute | solution.py:426
  1087.8 135.6 %collective-permute-start.73 = (f32[768,2048]{1,0:T(8,128)}, f32[768,2048]{1,0:T(8,128)}, u32[]{:S(2)}, u32[]{:S(2)}) collective-permute-start(f32[768,2048]{1,0:T(8,128)} %combine.4), channel_id=1, source_target_pairs={{16,8},{24,16},{17,9},{25,17},{18,10},{26,18},{19,11},{27,19},{20,... | collective-permute-start | bytes 18874376 | tf_op jit(solution)/shard_map/ppermute | solution.py:524
  1089.8 258.3 %collective-permute-start.60 = (f32[768,2048]{1,0:T(8,128)}, f32[768,2048]{1,0:T(8,128)}, u32[]{:S(2)}, u32[]{:S(2)}) collective-permute-start(f32[768,2048]{1,0:T(8,128)} %combine.4), channel_id=1, source_target_pairs={{0,8},{8,16},{1,9},{9,17},{2,10},{10,18},{3,11},{11,19},{4,12},{12... | collective-permute-start | bytes 18874376 | tf_op jit(solution)/shard_map/ppermute | solution.py:523
  1151.1 137.0 %collective-permute-start.46 = (bf16[4,216,2048]{2,1,0:T(8,128)(2,1)}, bf16[4,216,2048]{2,1,0:T(8,128)(2,1)}, u32[]{:S(2)}, u32[]{:S(2)}) collective-permute-start(bf16[4,216,2048]{2,1,0:T(8,128)(2,1)} %get-tuple-element.31), channel_id=1, source_target_pairs={{0,2},{1,3},{2,0},{3,1},{4,6},{5,7},{6,4},{7,5},{8,10},{9,11},{10,... | collective-permute-start | bytes 10616840 | tf_op jit(solution)/shard_map/ppermute | solution.py:426
  1217.3 130.7 %collective-permute-start.47 = (bf16[4,216,2048]{2,1,0:T(8,128)(2,1)}, bf16[4,216,2048]{2,1,0:T(8,128)(2,1)}, u32[]{:S(2)}, u32[]{:S(2)}) collective-permute-start(bf16[4,216,2048]{2,1,0:T(8,128)(2,1)} %get-tuple-element.32), channel_id=1, source_target_pairs={{0,4},{1,5},{2,6},{3,7},{4,0},{5,1},{6,2},{7,3},{8,12},{9,13},{10,... | collective-permute-start | bytes 10616840 | tf_op jit(solution)/shard_map/ppermute | solution.py:426
  1217.3 130.7 %collective-permute-start.48 = (bf16[4,216,2048]{2,1,0:T(8,128)(2,1)}, bf16[4,216,2048]{2,1,0:T(8,128)(2,1)}, u32[]{:S(2)}, u32[]{:S(2)}) collective-permute-start(bf16[4,216,2048]{2,1,0:T(8,128)(2,1)} %get-tuple-element.33), channel_id=1, source_target_pairs={{0,6},{1,7},{2,4},{3,5},{4,2},{5,3},{6,0},{7,1},{8,14},{9,15},{10,... | collective-permute-start | bytes 10616840 | tf_op jit(solution)/shard_map/ppermute | solution.py:426
  1248.1 342.8 %collective-permute-start.74 = (f32[768,2048]{1,0:T(8,128)}, f32[768,2048]{1,0:T(8,128)}, u32[]{:S(2)}, u32[]{:S(2)}) collective-permute-start(f32[768,2048]{1,0:T(8,128)} %combine.7), channel_id=1, source_target_pairs={{0,24},{8,0},{16,8},{24,16},{1,25},{9,1},{17,9},{25,17},{2,26},{10... | collective-permute-start | bytes 18874376 | tf_op jit(solution)/shard_map/ppermute | solution.py:432
  1370.1 135.8 %collective-permute-start.61 = (f32[768,2048]{1,0:T(8,128)}, f32[768,2048]{1,0:T(8,128)}, u32[]{:S(2)}, u32[]{:S(2)}) collective-permute-start(f32[768,2048]{1,0:T(8,128)} %combine.5), channel_id=1, source_target_pairs={{0,8},{8,16},{16,24},{24,0},{1,9},{9,17},{17,25},{25,1},{2,10},{10... | collective-permute-start | bytes 18874376 | tf_op jit(solution)/shard_map/ppermute | solution.py:432
  1430.0 86.0 %collective-permute-start.35 = (bf16[4,216,2048]{2,1,0:T(8,128)(2,1)}, bf16[4,216,2048]{2,1,0:T(8,128)(2,1)}, u32[]{:S(2)}, u32[]{:S(2)}) collective-permute-start(bf16[4,216,2048]{2,1,0:T(8,128)(2,1)} %get-tuple-element.26), channel_id=1, source_target_pairs={{0,2},{1,3},{2,0},{3,1},{4,6},{5,7},{6,4},{7,5},{8,10},{9,11},{10,... | collective-permute-start | bytes 10616840 | tf_op jit(solution)/shard_map/ppermute | solution.py:426
  1446.0 120.9 %collective-permute-start.36 = (bf16[4,216,2048]{2,1,0:T(8,128)(2,1)}, bf16[4,216,2048]{2,1,0:T(8,128)(2,1)}, u32[]{:S(2)}, u32[]{:S(2)}) collective-permute-start(bf16[4,216,2048]{2,1,0:T(8,128)(2,1)} %get-tuple-element.27), channel_id=1, source_target_pairs={{0,4},{1,5},{2,6},{3,7},{4,0},{5,1},{6,2},{7,3},{8,12},{9,13},{10,... | collective-permute-start | bytes 10616840 | tf_op jit(solution)/shard_map/ppermute | solution.py:426
  1461.1 107.7 %collective-permute-start.37 = (bf16[4,216,2048]{2,1,0:T(8,128)(2,1)}, bf16[4,216,2048]{2,1,0:T(8,128)(2,1)}, u32[]{:S(2)}, u32[]{:S(2)}) collective-permute-start(bf16[4,216,2048]{2,1,0:T(8,128)(2,1)} %get-tuple-element.28), channel_id=1, source_target_pairs={{0,6},{1,7},{2,4},{3,5},{4,2},{5,3},{6,0},{7,1},{8,14},{9,15},{10,... | collective-permute-start | bytes 10616840 | tf_op jit(solution)/shard_map/ppermute | solution.py:426
  (67 other events, 4397.9 us)
